TPU v7x, 32 devices: a whole 2x2x4 slice. The times are simulated.
32 devices in a mesh: band: 8 (over z, x), lev: 4 (over y, core).
Axes of the slice: x: 2, y: 2, z: 4, core: 2. Of those that a mesh axis runs over, the one named last changes fastest.
Arguments:
- checkpoints: float32 [4, 4, 32, 2, 256, 256], P(None, None, 'lev', None, 'band'), may hold values from -0.4 to 0.4
- final_cot: float32 [4, 32, 2, 256, 256], P(None, 'lev', None, 'band'), may hold values from -6 to 6
- obs_cot: float32 [4, 4, 32, 256, 512], P(None, None, None, 'band', 'lev'), may hold values from -0.2 to 0.2
- obs_time: int32 [4], replicated, may hold values from 0 to 3
- wave_order: int32 [256], replicated, may hold values from 0 to 255, each once
- legendre: bfloat16 [256, 256, 256], P('band'), may hold values from -0.375 to 0.375
- w_in: bfloat16 [128, 512], replicated, may hold values from -0.5 to 0.5
- w_out: bfloat16 [512, 128], replicated, may hold values from -0.25 to 0.25
- bias: float32 [512], replicated, may hold values from -3 to 3
Outputs:
- grad_state: float32 [4, 32, 2, 256, 256], P(None, 'lev', None, 'band')
- grad_w_in: float32 [128, 512], replicated
- grad_w_out: float32 [512, 128], replicated
- grad_bias: float32 [512], replicated
Inputs may be any that keep to these rules, and one draw needn't show every extreme that they name: `obs_time`: each number names a step of the rollout. `wave_order`: each of the 256 zonal wavenumbers once.
All inputs are finite; a program needn't handle non-finite values.
Results may differ from a plain program's by a relative error of at most 0.014.
Values may be sent and summed in bfloat16 or wider, within the bound.
A program may use at most 192 MiB of HBM per device.

v0:
```python
import jax
import jax.numpy as jnp
from jax import lax
from jax.sharding import PartitionSpec as P

dt_scale = 1.0


def tables(wave_order, lon_count):
    longitude = jnp.arange(lon_count, dtype=jnp.int32)
    phase_index = wave_order[:, None] * longitude[None, :] % lon_count
    angles = 2.0 * jnp.pi / lon_count * phase_index.astype(jnp.float32)
    return (jnp.cos(angles).astype(jnp.bfloat16), jnp.sin(angles).astype(jnp.bfloat16))


def rows_to_bands(sums, band_count):
    waves, lat, parts, steps, fields = sums.shape
    sums = sums.reshape(waves, band_count, lat // band_count, parts, steps, fields)
    return sums.transpose(1, 0, 3, 4, 2, 5).reshape(band_count, waves * parts, -1)


def synth_legendre(masked, spectral):
    return jnp.einsum(
        "rjn,svcrn->rjcsv",
        masked,
        spectral.astype(jnp.bfloat16),
        preferred_element_type=jnp.float32,
    ).astype(jnp.bfloat16)


def to_columns(masked, spectral, table, band_count, level_count, local_lat):
    steps, fields, local_levels = spectral.shape[:3]
    flat = spectral.reshape((steps, fields * local_levels) + spectral.shape[3:])
    sums = rows_to_bands(synth_legendre(masked, flat), band_count)
    rows = lax.all_to_all(sums, "band", split_axis=0, concat_axis=0, tiled=True)
    rows = rows.reshape(table.shape[0], -1)
    grid = jnp.einsum("kx,ko->xo", rows, table, preferred_element_type=jnp.float32).astype(
        jnp.bfloat16
    )
    grid = grid.reshape(steps, local_lat, fields * local_levels, level_count, -1)
    grid = grid.transpose(3, 0, 1, 2, 4)
    cols = lax.all_to_all(grid, "lev", split_axis=0, concat_axis=0, tiled=True)
    cols = cols.reshape(level_count, steps, local_lat, fields, local_levels, -1)
    cols = cols.transpose(1, 2, 3, 0, 4, 5)
    return cols.reshape(steps, local_lat, fields * level_count * local_levels, -1)


def network_grads(features, tangent, w_in, w_out, bias):
    preact = jnp.einsum("fh,jfo->jho", w_in, features, preferred_element_type=jnp.float32)
    preact = preact + bias[None, :, None]
    logistic = jax.nn.sigmoid(preact)
    hidden = (preact * logistic).astype(jnp.bfloat16)
    hidden_grad = jnp.einsum("hf,jfo->jho", w_out, tangent, preferred_element_type=jnp.float32)
    preact_grad = hidden_grad * (logistic * (1.0 + preact * (1.0 - logistic)))
    preact_low = preact_grad.astype(jnp.bfloat16)
    out_grad = jnp.einsum("jho,jfo->hf", hidden, tangent, preferred_element_type=jnp.float32)
    in_grad = jnp.einsum("jfo,jho->fh", features, preact_low, preferred_element_type=jnp.float32)
    bias_grad = jnp.sum(preact_grad, axis=(0, 2))
    column_grad = jnp.einsum("fh,jho->fjo", w_in, preact_low, preferred_element_type=jnp.float32)
    return (in_grad, out_grad, bias_grad, column_grad)


def reduce_grads(in_grad, out_grad, bias_grad):
    axes = ("band", "lev")
    devices = lax.axis_size(axes)
    feature_count, hidden_count = in_grad.shape
    rows = 2 * feature_count + 1
    padding = -rows % devices
    packed = jnp.concatenate(
        [
            in_grad,
            out_grad.T,
            bias_grad[None],
            jnp.zeros((padding, hidden_count), jnp.float32),
        ]
    )
    packed = packed.reshape(devices, -1, hidden_count)
    parts = lax.all_to_all(packed, axes, split_axis=0, concat_axis=0, tiled=True)
    total = lax.all_gather(jnp.sum(parts, axis=0), axes, axis=0, tiled=True)
    return (
        total[:feature_count],
        total[feature_count : 2 * feature_count].T,
        total[2 * feature_count],
    )


def shards(checkpoints, final_cot, obs_cot, obs_time, wave_order, legendre, w_in, w_out, bias):
    level_count = lax.axis_size("lev")
    band_count = lax.axis_size("band")
    local_waves, lat_count, wave_count = legendre.shape
    field_count, local_levels = final_cot.shape[:2]
    local_lat, local_lon = obs_cot.shape[3:]
    lon_count = local_lon * level_count
    step_count = checkpoints.shape[0]
    row_start = lax.axis_index("band") * local_waves
    my_waves = lax.dynamic_slice_in_dim(wave_order, row_start, local_waves)
    degrees = jnp.arange(wave_count, dtype=jnp.int32)
    upper_mask = degrees[None, None, :] >= my_waves[:, None, None]
    masked = jnp.where(upper_mask, legendre, jnp.zeros_like(legendre))
    cosine_table, sine_table = tables(wave_order, lon_count)
    table = jnp.stack([cosine_table, -sine_table], axis=1).reshape(2 * wave_count, lon_count)
    weight_m = jnp.where(wave_order == 0, 1.0, 2.0).astype(jnp.bfloat16)
    state_table = table * jnp.repeat(weight_m, 2)[:, None]
    tangent_table = table * jnp.asarray(1.0 / lon_count, jnp.bfloat16)
    degree_float = degrees.astype(jnp.float32)
    damping = 1.0 / (1.0 + 2.0 * degree_float * (degree_float + 1.0) / (wave_count * wave_count))
    state_columns = to_columns(
        masked, checkpoints, state_table, band_count, level_count, local_lat
    )
    adjoint = final_cot
    grads = None
    for step in reversed(range(step_count)):
        damped = damping * adjoint
        tangent = to_columns(
            masked, dt_scale * damped[None], tangent_table, band_count, level_count, local_lat
        )[0]
        in_grad, out_grad, bias_grad, column_grad = network_grads(
            state_columns[step], tangent, w_in, w_out, bias
        )
        new = (in_grad, out_grad, bias_grad)
        grads = new if grads is None else tuple(x + y for x, y in zip(grads, new))
        obs_sum = sum(
            jnp.where(obs_time[i] == step, obs_cot[i], 0.0) for i in range(obs_cot.shape[0])
        )
        column_grad = column_grad.reshape(obs_sum.shape) + obs_sum
        column_grad = column_grad.astype(jnp.bfloat16).reshape(
            field_count, level_count, local_levels, local_lat, local_lon
        )
        send = column_grad.transpose(1, 0, 2, 3, 4)
        level_grad = lax.all_to_all(send, "lev", split_axis=0, concat_axis=0, tiled=True)
        level_grad = level_grad.transpose(1, 2, 3, 0, 4).reshape(-1, lon_count)
        back = jnp.einsum(
            "ko,xo->kx", state_table, level_grad, preferred_element_type=jnp.float32
        ).astype(jnp.bfloat16)
        back = back.reshape(band_count, 2 * local_waves, -1)
        back = lax.all_to_all(back, "band", split_axis=0, concat_axis=0, tiled=True)
        back = back.reshape(
            band_count, local_waves, 2, field_count, local_levels, local_lat
        )
        back = back.transpose(1, 2, 3, 4, 0, 5).reshape(
            local_waves, 2, field_count, local_levels, lat_count
        )
        adjoint = damped + jnp.einsum(
            "rjn,rcvlj->vlcrn", masked, back, preferred_element_type=jnp.float32
        )
    return (adjoint,) + reduce_grads(*grads)


def solution(mesh):
    placed = (
        P(None, None, "lev", None, "band", None),
        P(None, "lev", None, "band", None),
        P(None, None, None, "band", "lev"),
        P(),
        P(),
        P("band", None, None),
        P(),
        P(),
        P(),
    )
    return jax.shard_map(
        shards,
        mesh=mesh,
        in_specs=placed,
        out_specs=(P(None, "lev", None, "band", None), P(), P(), P()),
        check_vma=False,
    )
```

profile of v0, /device:TPU:1, one launch (start us, length us, event | category | flops | bytes accessed | tf_op | source)
XLA Modules:
  0.0 925.0 jit_solution(16788949452792766176)
XLA Ops:
  9.3 6.8 copy.317
  16.2 7.0 reshape.613
  23.2 6.3 all-to-all-start
  34.1 4.7 convert_bitcast_fusion
  38.8 18.7 %reshape.617 = bf16[32,8,32,2,4,32]{2,1,5,3,4,0:T(8,128)(2,1)} reshape(bf16[32,256,2,4,32]{1,4,2,3,0:T(8,128)(2,1)} %convert_bitcast_fusion) | data formatting | bytes 8388608 | tf_op jit(solution)/shard_map/reshape | solution.py:18
  57.5 22.7 %copy.323 = bf16[32,8,32,2,4,32]{5,2,4,3,0,1:T(8,128)(2,1)} copy(bf16[32,8,32,2,4,32]{2,1,5,3,4,0:T(8,128)(2,1)} %reshape.617) | data formatting | bytes 8388608 | tf_op jit(solution)/shard_map/reshape | solution.py:18
  80.2 21.7 %reshape.618 = bf16[8,64,4096]{2,1,0:T(8,128)(2,1)} reshape(bf16[8,32,2,4,32,32]{5,4,3,2,1,0:T(8,128)(2,1)} %bitcast.492) | data formatting | bytes 8388608 | tf_op jit(solution)/shard_map/reshape | solution.py:19
  101.9 5.8 all-to-all-start.2
  118.0 81.6 %all-to-all-done.2 = bf16[8,64,4096]{2,1,0:T(8,128)(2,1)} async-done(((bf16[8,64,4096]{2,1,0:T(8,128)(2,1)}), bf16[8,64,4096]{2,1,0:T(8,128)(2,1)}, u32[]{:S(2)}, u32[]{:S(2)}) %all-to-all-start.2) | async-done | bytes 4194336 | tf_op jit(solution)/shard_map/all_to_all | solution.py:35
  199.6 5.8 all-to-all-start.1
  206.2 6.8 convolution_convert_fusion
  213.0 6.9 reshape.620
  219.9 5.0 copy.462
  224.9 5.4 all-to-all-start.3
  236.3 6.0 select_add_fusion.2
  243.6 34.0 %all-to-all-done.3 = bf16[4,4,32,32,128]{4,3,2,1,0:T(8,128)(2,1)} async-done(((bf16[4,4,32,32,128]{4,3,2,1,0:T(8,128)(2,1)}), bf16[4,4,32,32,128]{4,3,2,1,0:T(8,128)(2,1)}, u32[]{:S(2)}, u32[]{:S(2)}) %all-to-all-start.3) | async-done | bytes 4194336 | tf_op jit(solution)/shard_map/all_to_all | solution.py:42
  290.6 16.9 %all_to_all.95 = bf16[4,4,8,32,128]{4,3,2,1,0:T(8,128)(2,1)S(1)} all-to-all(bf16[4,4,8,32,128]{4,3,2,1,0:T(8,128)(2,1)S(1)} %copy.329), channel_id=1, replica_groups=mesh['band'=8,'lev'=4] {'lev'}, dimensions={0} | all-to-all | bytes 2097152 | tf_op jit(solution)/shard_map/all_to_all | solution.py:130
  309.2 28.3 %all_to_all.96 = bf16[8,64,1024]{2,1,0:T(8,128)(2,1)S(1)} all-to-all(bf16[8,64,1024]{2,1,0:T(8,128)(2,1)S(1)} %bitcast.540), channel_id=1, replica_groups=mesh['band'=8,'lev'=4] {'band'}, dimensions={0} | all-to-all | bytes 2097152 | tf_op jit(solution)/shard_map/all_to_all | solution.py:136
  341.7 11.9 %copy.461 = bf16[8,32,2,4,8,32]{5,0,4,3,2,1:T(8,128)(2,1)} copy(bf16[8,32,2,4,8,32]{5,4,3,2,1,0:T(8,128)(2,1)} %reshape.625) | data formatting | bytes 2097152 | tf_op jit(solution)/shard_map/reshape | solution.py:137
  353.6 6.4 reshape.626
  360.0 5.0 fusion.61
  367.5 5.8 reshape.627
  373.3 6.8 copy.332
  380.1 7.0 reshape.628
  387.1 28.9 %all_to_all.97 = bf16[8,64,1024]{2,1,0:T(8,128)(2,1)S(1)} all-to-all(bf16[8,64,1024]{2,1,0:T(8,128)(2,1)} %reshape.628), channel_id=1, replica_groups=mesh['band'=8,'lev'=4] {'band'}, dimensions={0} | all-to-all | bytes 2097152 | tf_op jit(solution)/shard_map/all_to_all | solution.py:35
  423.4 6.3 all-to-all-start.7
  432.2 4.6 fusion.194
  436.8 6.5 all-to-all-done.7
  444.8 6.8 fusion.222
  456.0 16.9 %all_to_all.98 = bf16[4,4,8,32,128]{4,3,2,1,0:T(8,128)(2,1)S(1)} all-to-all(bf16[4,4,8,32,128]{4,3,2,1,0:T(8,128)(2,1)S(1)} %copy.340), channel_id=1, replica_groups=mesh['band'=8,'lev'=4] {'lev'}, dimensions={0} | all-to-all | bytes 2097152 | tf_op jit(solution)/shard_map/all_to_all | solution.py:130
  474.6 28.6 %all_to_all.99 = bf16[8,64,1024]{2,1,0:T(8,128)(2,1)} all-to-all(bf16[8,64,1024]{2,1,0:T(8,128)(2,1)S(1)} %bitcast.543), channel_id=1, replica_groups=mesh['band'=8,'lev'=4] {'band'}, dimensions={0} | all-to-all | bytes 2097152 | tf_op jit(solution)/shard_map/all_to_all | solution.py:136
  503.1 6.2 reshape.635
  509.4 11.8 %copy.460 = bf16[8,32,2,4,8,32]{5,0,4,3,2,1:T(8,128)(2,1)} copy(bf16[8,32,2,4,8,32]{5,4,3,2,1,0:T(8,128)(2,1)} %reshape.635) | data formatting | bytes 2097152 | tf_op jit(solution)/shard_map/reshape | solution.py:137
  521.2 6.3 reshape.636
  537.0 6.8 copy.343
  543.8 7.0 reshape.638
  560.0 19.4 %all-to-all-done.10 = bf16[8,64,1024]{2,1,0:T(8,128)(2,1)S(1)} async-done(((bf16[8,64,1024]{2,1,0:T(8,128)(2,1)}), bf16[8,64,1024]{2,1,0:T(8,128)(2,1)S(1)}, u32[]{:S(2)}, u32[]{:S(2)}) %all-to-all-start.10) | async-done | bytes 1048608 | tf_op jit(solution)/shard_map/all_to_all | solution.py:35
  582.7 6.5 all-to-all-start.11
  589.2 6.1 select_add_fusion
  596.6 4.6 fusion.191
  604.3 6.7 fusion.220
  614.0 16.9 %all_to_all.100 = bf16[4,4,8,32,128]{4,3,2,1,0:T(8,128)(2,1)S(1)} all-to-all(bf16[4,4,8,32,128]{4,3,2,1,0:T(8,128)(2,1)S(1)} %copy.351), channel_id=1, replica_groups=mesh['band'=8,'lev'=4] {'lev'}, dimensions={0} | all-to-all | bytes 2097152 | tf_op jit(solution)/shard_map/all_to_all | solution.py:130
  641.1 4.5 fusion.188
  645.7 16.3 %all-to-all-done.13 = bf16[8,64,1024]{2,1,0:T(8,128)(2,1)S(1)} async-done(((bf16[8,64,1024]{2,1,0:T(8,128)(2,1)}), bf16[8,64,1024]{2,1,0:T(8,128)(2,1)S(1)}, u32[]{:S(2)}, u32[]{:S(2)}) %all-to-all-start.13) | async-done | bytes 1048608 | tf_op jit(solution)/shard_map/all_to_all | solution.py:136
  666.3 11.8 %copy.459 = bf16[8,32,2,4,8,32]{5,0,4,3,2,1:T(8,128)(2,1)} copy(bf16[8,32,2,4,8,32]{5,4,3,2,1,0:T(8,128)(2,1)} %reshape.645) | data formatting | bytes 2097152 | tf_op jit(solution)/shard_map/reshape | solution.py:137
  678.0 5.5 reshape.646
  692.4 6.9 copy.354
  699.2 7.1 reshape.648
  706.3 4.9 all-to-all-start.14
  711.3 6.8 fusion.133
  719.5 6.7 fusion.130
  726.3 9.7 %all-to-all-done.14 = bf16[8,64,1024]{2,1,0:T(8,128)(2,1)} async-done(((bf16[8,64,1024]{2,1,0:T(8,128)(2,1)}), bf16[8,64,1024]{2,1,0:T(8,128)(2,1)}, u32[]{:S(2)}, u32[]{:S(2)}) %all-to-all-start.14) | async-done | bytes 1048608 | tf_op jit(solution)/shard_map/all_to_all | solution.py:35
  741.5 6.0 all-to-all-start.15
  747.5 7.1 fusion.142
  755.4 5.6 all-to-all-done.15
  761.2 6.6 fusion.219
  767.8 8.2 fusion.145
  779.9 5.2 all-to-all-start.16
  790.0 8.7 all-to-all-done.16
  806.7 20.5 %all-to-all-done.18 = f32[32,9,512]{2,1,0:T(8,128)S(1)} async-done(((f32[32,9,512]{2,1,0:T(8,128)}), f32[32,9,512]{2,1,0:T(8,128)S(1)}, u32[]{:S(2)}, u32[]{:S(2)}) %all-to-all-start.18) | async-done | bytes 589856 | tf_op jit(solution)/shard_map/all_to_all | solution.py:78
  833.6 57.7 %all-gather = f32[32,9,512]{2,1,0:T(8,128)} all-gather(f32[1,9,512]{2,1,0:T(8,128)S(1)} %bitcast.545), channel_id=1, replica_groups=mesh['band'=8,'lev'=4] {'band','lev'}, dimensions={0}, use_global_device_ids=true | all-gather | bytes 608256 | tf_op jit(solution)/shard_map/all_gather | solution.py:79
  897.3 4.6 reshape.655
  901.9 11.8 %copy.458 = bf16[8,32,2,4,8,32]{5,0,4,3,2,1:T(8,128)(2,1)} copy(bf16[8,32,2,4,8,32]{5,4,3,2,1,0:T(8,128)(2,1)} %reshape.655) | data formatting | bytes 2097152 | tf_op jit(solution)/shard_map/reshape | solution.py:137
  913.7 5.3 reshape.656
  (181 shorter events, 154.7 us)
Async XLA Ops:
  0.6 281.5 %copy-start = (bf16[128,512]{1,0:T(8,128)(2,1)S(1)}, bf16[128,512]{1,0:T(8,128)(2,1)}, u32[]{:S(2)}) copy-start(bf16[128,512]{1,0:T(8,128)(2,1)} %param.15) | copy-start | bytes 393220
  23.2 78.8 %all-to-all-start = ((bf16[8,64,1024]{2,1,0:T(8,128)(2,1)}), bf16[8,64,1024]{2,1,0:T(8,128)(2,1)S(1)}, u32[]{:S(2)}, u32[]{:S(2)}) async-start(bf16[8,64,1024]{2,1,0:T(8,128)(2,1)} %reshape.613), calls=%async_computation | async-start | bytes 2097152 | tf_op jit(solution)/shard_map/all_to_all | solution.py:35
  29.5 4.6 copy-start.1
  101.9 5.9 copy-start.38
  101.9 97.7 %all-to-all-start.2 = ((bf16[8,64,4096]{2,1,0:T(8,128)(2,1)}), bf16[8,64,4096]{2,1,0:T(8,128)(2,1)}, u32[]{:S(2)}, u32[]{:S(2)}) async-start(bf16[8,64,4096]{2,1,0:T(8,128)(2,1)} %reshape.618), calls=%async_computation.2 | async-start | bytes 8388608 | tf_op jit(solution)/shard_map/all_to_all | solution.py:35
  113.0 0.8 copy-start.34
  199.6 25.3 %all-to-all-start.1 = ((bf16[4,1,32,32,128]{4,3,2,1,0:T(8,128)(2,1)}), bf16[4,1,32,32,128]{4,3,2,1,0:T(8,128)(2,1)S(1)}, u32[]{:S(2)}, u32[]{:S(2)}) async-start(bf16[4,1,32,32,128]{4,3,2,1,0:T(8,128)(2,1)} %bitcast.491), calls=%async_computation.1 | async-start | bytes 2097152 | tf_op jit(solution)/shard_map/all_to_all | solution.py:42
  206.2 6.8 copy-start.30
  224.9 5.4 copy-start.37
  224.9 52.7 %all-to-all-start.3 = ((bf16[4,4,32,32,128]{4,3,2,1,0:T(8,128)(2,1)}), bf16[4,4,32,32,128]{4,3,2,1,0:T(8,128)(2,1)}, u32[]{:S(2)}, u32[]{:S(2)}) async-start(bf16[4,4,32,32,128]{4,3,2,1,0:T(8,128)(2,1)} %bitcast.501), calls=%async_computation.3 | async-start | bytes 8388608 | tf_op jit(solution)/shard_map/all_to_all | solution.py:42
  282.1 1.3 copy-start.25
  282.1 1.3 copy-start.40
  282.1 1.3 copy-start.41
  283.4 4.3 copy-start.18
  287.7 2.8 copy-start.6
  290.5 17.9 %copy-start.31 = (bf16[512,512]{1,0:T(8,128)(2,1)S(1)}, bf16[512,512]{1,0:T(8,128)(2,1)}, u32[]{:S(2)}) copy-start(bf16[512,512]{1,0:T(8,128)(2,1)} %copy-done.30) | copy-start | bytes 1572868
  360.0 5.0 copy-start.2
  423.4 19.9 %all-to-all-start.7 = ((bf16[4,1,32,32,128]{4,3,2,1,0:T(8,128)(2,1)}), bf16[4,1,32,32,128]{4,3,2,1,0:T(8,128)(2,1)}, u32[]{:S(2)}, u32[]{:S(2)}) async-start(bf16[4,1,32,32,128]{4,3,2,1,0:T(8,128)(2,1)} %bitcast.522), calls=%async_computation.7 | async-start | bytes 2097152 | tf_op jit(solution)/shard_map/all_to_all | solution.py:42
  431.3 1.0 copy-start.12
  444.8 6.8 copy-start.26
  451.6 4.4 copy-start.7
  451.6 3.1 copy-start.20
  455.9 17.9 %copy-start.32 = (bf16[512,512]{1,0:T(8,128)(2,1)S(1)}, bf16[512,512]{1,0:T(8,128)(2,1)}, u32[]{:S(2)}) copy-start(bf16[512,512]{1,0:T(8,128)(2,1)} %copy-done.30) | copy-start | bytes 1572868
  527.5 4.8 copy-start.3
  531.0 1.3 copy-start.5
  550.8 28.6 %all-to-all-start.10 = ((bf16[8,64,1024]{2,1,0:T(8,128)(2,1)}), bf16[8,64,1024]{2,1,0:T(8,128)(2,1)S(1)}, u32[]{:S(2)}, u32[]{:S(2)}) async-start(bf16[8,64,1024]{2,1,0:T(8,128)(2,1)} %reshape.638), calls=%async_computation.10 | async-start | bytes 2097152 | tf_op jit(solution)/shard_map/all_to_all | solution.py:35
  582.7 20.1 %all-to-all-start.11 = ((bf16[4,1,32,32,128]{4,3,2,1,0:T(8,128)(2,1)}), bf16[4,1,32,32,128]{4,3,2,1,0:T(8,128)(2,1)}, u32[]{:S(2)}, u32[]{:S(2)}) async-start(bf16[4,1,32,32,128]{4,3,2,1,0:T(8,128)(2,1)} %bitcast.489), calls=%async_computation.11 | async-start | bytes 2097152 | tf_op jit(solution)/shard_map/all_to_all | solution.py:42
  589.2 6.1 copy-start.23
  595.6 1.0 copy-start.16
  604.3 6.8 copy-start.28
  611.0 2.8 copy-start.9
  613.9 17.8 %copy-start.33 = (bf16[512,512]{1,0:T(8,128)(2,1)S(1)}, bf16[512,512]{1,0:T(8,128)(2,1)}, u32[]{:S(2)}) copy-start(bf16[512,512]{1,0:T(8,128)(2,1)} %copy-done.30) | copy-start | bytes 1572868
  614.0 23.6 %copy-start.22 = (bf16[1,32,4,4,8,128]{5,4,2,1,0,3:T(8,128)(2,1)S(1)}, bf16[1,32,4,4,8,128]{5,4,2,1,0,3:T(8,128)(2,1)}, u32[]{:S(2)}) copy-start(bf16[1,32,4,4,8,128]{5,4,2,1,0,3:T(8,128)(2,1)} %get-tuple-element.36) | copy-start | bytes 3145732
  633.5 28.5 %all-to-all-start.13 = ((bf16[8,64,1024]{2,1,0:T(8,128)(2,1)}), bf16[8,64,1024]{2,1,0:T(8,128)(2,1)S(1)}, u32[]{:S(2)}, u32[]{:S(2)}) async-start(bf16[8,64,1024]{2,1,0:T(8,128)(2,1)} %bitcast.535), calls=%async_computation.13 | async-start | bytes 2097152 | tf_op jit(solution)/shard_map/all_to_all | solution.py:136
  637.8 3.3 copy-start.14
  683.6 4.1 copy-start.4
  699.2 12.0 %copy-start.27 = (bf16[1,32,4,4,8,128]{5,4,3,2,1,0:T(8,128)(2,1)S(1)}, bf16[1,32,4,4,8,128]{5,4,3,2,1,0:T(8,128)(2,1)}, u32[]{:S(2)}) copy-start(bf16[1,32,4,4,8,128]{5,4,3,2,1,0:T(8,128)(2,1)} %copy-done.26) | copy-start | bytes 3145732
  699.2 12.0 %copy-start.42 = (f32[512]{0:T(512)S(1)}, f32[512]{0:T(512)}, u32[]{:S(2)}) copy-start(f32[512]{0:T(512)} %param.17) | copy-start | bytes 6148
  706.3 29.7 %all-to-all-start.14 = ((bf16[8,64,1024]{2,1,0:T(8,128)(2,1)}), bf16[8,64,1024]{2,1,0:T(8,128)(2,1)}, u32[]{:S(2)}, u32[]{:S(2)}) async-start(bf16[8,64,1024]{2,1,0:T(8,128)(2,1)} %reshape.648), calls=%async_computation.14 | async-start | bytes 2097152 | tf_op jit(solution)/shard_map/all_to_all | solution.py:35
  711.3 6.8 copy-start.8
  711.3 6.8 copy-start.13
  718.1 1.4 copy-start.29
  719.5 16.5 %copy-start.35 = (bf16[512,512]{1,0:T(8,128)(2,1)S(1)}, bf16[512,512]{1,0:T(8,128)(2,1)}, u32[]{:S(2)}) copy-start(bf16[512,512]{1,0:T(8,128)(2,1)} %copy-done.34) | copy-start | bytes 1572868
  736.0 11.5 %copy-start.43 = (f32[128,512]{1,0:T(8,128)S(1)}, f32[128,512]{1,0:T(8,128)}, u32[]{:S(2)}) copy-start(f32[128,512]{1,0:T(8,128)} %fusion.133) | copy-start | bytes 786436
  741.5 19.4 %all-to-all-start.15 = ((bf16[4,1,32,32,128]{4,3,2,1,0:T(8,128)(2,1)}), bf16[4,1,32,32,128]{4,3,2,1,0:T(8,128)(2,1)S(1)}, u32[]{:S(2)}, u32[]{:S(2)}) async-start(bf16[4,1,32,32,128]{4,3,2,1,0:T(8,128)(2,1)} %bitcast.521), calls=%async_computation.15 | async-start | bytes 2097152 | tf_op jit(solution)/shard_map/all_to_all | solution.py:42
  747.5 7.1 copy-start.10
  747.5 7.1 copy-start.17
  747.5 7.1 copy-start.24
  761.2 6.6 copy-start.44
  767.8 8.2 copy-start.11
  776.0 1.6 copy-start.19
  777.5 7.5 copy-start.39
  777.5 8.3 copy-start.15
  779.9 18.8 %all-to-all-start.16 = ((bf16[4,4,8,32,128]{4,3,2,1,0:T(8,128)(2,1)}), bf16[4,4,8,32,128]{4,3,2,1,0:T(8,128)(2,1)}, u32[]{:S(2)}, u32[]{:S(2)}) async-start(bf16[4,4,8,32,128]{4,3,2,1,0:T(8,128)(2,1)} %copy.362), calls=%async_computation.16 | async-start | bytes 2097152 | tf_op jit(solution)/shard_map/all_to_all | solution.py:130
  785.1 3.7 copy-start.36
  798.6 28.6 %all-to-all-start.18 = ((f32[32,9,512]{2,1,0:T(8,128)}), f32[32,9,512]{2,1,0:T(8,128)S(1)}, u32[]{:S(2)}, u32[]{:S(2)}) async-start(f32[32,9,512]{2,1,0:T(8,128)} %reshape.657), calls=%async_computation.18 | async-start | bytes 2097152 | tf_op jit(solution)/shard_map/all_to_all | solution.py:78
  827.2 1.0 copy-start.21
  828.2 69.1 %all-to-all-start.17 = ((bf16[8,64,1024]{2,1,0:T(8,128)(2,1)}), bf16[8,64,1024]{2,1,0:T(8,128)(2,1)S(1)}, u32[]{:S(2)}, u32[]{:S(2)}) async-start(bf16[8,64,1024]{2,1,0:T(8,128)(2,1)} %bitcast.533), calls=%async_computation.17 | async-start | bytes 2097152 | tf_op jit(solution)/shard_map/all_to_all | solution.py:136
where the time goes:
time: 938 us; the launch traced here: 925 us
  local copies, waits for them, and re-layouts  285 us (30%)
  waiting for transfers between devices  204 us (22%)
  blocking collectives  194 us (21%)
  matrix products  134 us (14%)
  starting transfers between devices  67.6 us (7%)
  other arithmetic  28.2 us (3%)
  between operations  12.3 us (1%)
    all_to_all x4, waiting for transfers between devices, to_columns(): rows = lax.all_to_all(sums, 'band', split_axis=0, concat_axis=0, tiled=True)  111 us
    reshape x10, local copies, waits for them, and re-layouts, rows_to_bands(): sums.reshape(waves, band_count, lat // band_count, parts, steps, fields)  84.5 us
    reshape x8, local copies, waits for them, and re-layouts, shards(): back.reshape(band_count, local_waves, 2, field_count, local_levels, local...  66.7 us
    all_gather x1, blocking collectives, reduce_grads(): total = lax.all_gather(jnp.sum(parts, axis=0), axes, axis=0, tiled=True)  57.7 us
    all_to_all x2, blocking collectives, shards(): back = lax.all_to_all(back, 'band', split_axis=0, concat_axis=0, tiled=True)  56.8 us
    all_to_all x3, blocking collectives, shards(): lax.all_to_all(send, 'lev', split_axis=0, concat_axis=0, tiled=True)  50.8 us
    reshape x5, local copies, waits for them, and re-layouts, rows_to_bands(): sums.transpose(1, 0, 3, 4, 2, 5).reshape(band_count, waves * parts, -1)  49.8 us
    all_to_all x5, waiting for transfers between devices, to_columns(): cols = lax.all_to_all(grid, 'lev', split_axis=0, concat_axis=0, tiled=True)  47.6 us
  transfers between devices with their start and end apart: 13, of which 10 were waited for; matrix products, arithmetic and copies ran while one was open for 19% of the time, Pallas kernels for 0%

commit v1 on v0

v1 whole, which is shorter than its diff:
```python
import functools

import jax
import jax.numpy as jnp
from jax import lax
from jax.experimental import pallas as pl
from jax.experimental.pallas import tpu as pltpu
from jax.sharding import PartitionSpec as P

dt_scale = 1.0
F32 = jnp.float32
BF16 = jnp.bfloat16
MESH = pl.DeviceIdType.MESH
LANES = 128


def dot(a, b):
    return jnp.dot(a, b, preferred_element_type=F32)


def dot_nt(a, b):
    return lax.dot_general(a, b, (((1,), (1,)), ((), ())), preferred_element_type=F32)


class Sizes:
    def __init__(self, bands, levs, steps, fields, levels, waves, wave_count, lat, lon, nobs, hidden):
        self.B, self.LV, self.S, self.NO = bands, levs, steps, nobs
        self.V, self.L, self.R, self.N = fields, levels, waves, wave_count
        self.J, self.O, self.H = lat, lon, hidden
        self.RP = waves // 2
        self.RT = self.RP * bands
        self.JJ = min(16, lat)
        self.Q = lat // self.JJ
        self.VL = fields * levels
        self.C = 4 * self.VL
        self.F = self.VL * levs
        self.ND = bands * levs
        self.HD = hidden // self.ND
        self.PITCH = self.JJ + 8
        self.OPITCH = self.F + 8
        self.ROWS = self.VL * 2 * waves
        self.G = min(8, self.JJ)
        self.HC = min(256, hidden)


def kernel(
    z, ck, fc, obs, leg, obs_time, wave, damp, tab_t, tab_w, w_in_t, w_in, w_out, bias,
    out, gout,
    tab, adj, tsend, trecv, fsend, frecv, bsend, brecv,
    lf_send, lf_recv, lt_send, lt_recv, lg_send, lg_recv,
    fs, fs2, cstage, ostage, obs_all, obs_s, acc_in, acc_out, acc_b,
    rs_send, rs_recv, ag_send, ag_recv,
    t_s, t_r, f_s, f_r, b_s, b_r, lf_s, lf_r, lt_s, lt_r, lg_s, lg_r, rs_s, rs_r, ag_s, ag_r,
    ck_sem, fc_sem, obs_sem, leg_sem, out_sem, g_sem,
):
    me_b = lax.axis_index("band")
    me_l = lax.axis_index("lev")
    me = me_b * z.LV + me_l

    def to_band(src, dst, ssem, rsem, b):
        return pltpu.make_async_remote_copy(
            src_ref=src, dst_ref=dst, send_sem=ssem, recv_sem=rsem,
            device_id=(b, me_l), device_id_type=MESH,
        )

    def to_lev(src, dst, ssem, rsem, v):
        return pltpu.make_async_remote_copy(
            src_ref=src, dst_ref=dst, send_sem=ssem, recv_sem=rsem,
            device_id=(me_b, v), device_id_type=MESH,
        )

    def others(count, own, body):
        def step(d, _):
            body(lax.rem(own + d, count))
            return 0

        lax.fori_loop(1, count, step, 0)

    def band_send(send, recv, ssem, rsem, q):
        others(z.B, me_b, lambda b: to_band(
            send.at[b, q], recv.at[me_b, q], ssem.at[q, b], rsem.at[q, me_b], b).start())
        recv[me_b, q] = send[me_b, q]

    def band_wait_recv(send, recv, ssem, rsem, q):
        others(z.B, me_b, lambda b: to_band(
            send.at[b, q], recv.at[b, q], ssem.at[q, b], rsem.at[q, b], b).wait_recv())

    def band_wait_send(send, recv, ssem, rsem, q):
        others(z.B, me_b, lambda b: to_band(
            send.at[b, q], recv.at[b, q], ssem.at[q, b], rsem.at[q, b], b).wait_send())

    def feat_send(par):
        others(z.B, me_b, lambda b: to_band(
            fsend.at[b], frecv.at[par, me_b], f_s.at[b], f_r.at[par, me_b], b).start())
        frecv[par, me_b] = fsend[me_b]

    def feat_wait_recv(par):
        others(z.B, me_b, lambda b: to_band(
            fsend.at[b], frecv.at[par, b], f_s.at[b], f_r.at[par, b], b).wait_recv())

    def feat_wait_send():
        others(z.B, me_b, lambda b: to_band(
            fsend.at[b], frecv.at[0, b], f_s.at[b], f_r.at[0, b], b).wait_send())

    def lev_send(send, recv, ssem, rsem, q):
        others(z.LV, me_l, lambda v: to_lev(
            send.at[v, q], recv.at[me_l, q], ssem.at[q, v], rsem.at[q, me_l], v).start())
        recv[me_l, q] = send[me_l, q]

    def lev_wait_recv(send, recv, ssem, rsem, q):
        others(z.LV, me_l, lambda v: to_lev(
            send.at[v, q], recv.at[v, q], ssem.at[q, v], rsem.at[q, v], v).wait_recv())

    def lev_wait_send(send, recv, ssem, rsem, q):
        others(z.LV, me_l, lambda v: to_lev(
            send.at[v, q], recv.at[v, q], ssem.at[q, v], rsem.at[q, v], v).wait_send())

    def ck_copy(k, h):
        return pltpu.make_async_copy(
            ck.at[k, :, pl.ds(h * LANES, LANES)], cstage.at[h], ck_sem.at[h])

    def fc_copy(h):
        return pltpu.make_async_copy(
            fc.at[:, pl.ds(h * LANES, LANES)], ostage.at[h], fc_sem.at[h])

    def out_copy(h):
        return pltpu.make_async_copy(
            ostage.at[h], out.at[:, pl.ds(h * LANES, LANES)], out_sem.at[h])

    halves = z.N // LANES
    bj = z.B * z.JJ
    if z.Q == 1:
        leg_copies = [pltpu.make_async_copy(leg, tab.at[:, 0], leg_sem.at[0])]
    else:
        leg_copies = [
            pltpu.make_async_copy(
                leg.at[:, pl.ds(b * z.J + q * z.JJ, z.JJ), :],
                tab.at[:, q, pl.ds(b * z.JJ, z.JJ), :],
                leg_sem.at[b * z.Q + q],
            )
            for b in range(z.B)
            for q in range(z.Q)
        ]
    obs_copy = pltpu.make_async_copy(obs, obs_all, obs_sem.at[0])
    for h in range(halves):
        ck_copy(z.S - 1, h).start()
    for c in leg_copies:
        c.start()
    for h in range(halves):
        fc_copy(h).start()
    obs_copy.start()

    half_c = 2 * z.VL
    degree = lax.broadcasted_iota(jnp.int32, (half_c, z.N), 1)

    def upper(rp, r2):
        return degree >= wave[me_b * z.R + 2 * rp + r2]

    def rows_of(stage, rp):
        parts = []
        for r2 in range(2):
            for p in range(2):
                start = p * z.R + 2 * rp + r2
                parts.append(jnp.concatenate(
                    [stage[h, pl.ds(start, z.VL, stride=2 * z.R), :] for h in range(halves)], axis=1))
        return jnp.concatenate(parts, axis=0)

    lane = lax.broadcasted_iota(jnp.int32, (z.Q * bj, z.C), 1)

    def legendre(s, rp, send):
        masked = jnp.concatenate(
            [jnp.where(upper(rp, r2), s[r2 * half_c:(r2 + 1) * half_c], 0.0) for r2 in range(2)],
            axis=0).astype(BF16)
        sums = [dot_nt(tab[2 * rp + r2].reshape(z.Q * bj, z.N), masked) for r2 in range(2)]
        sums = jnp.where(lane < half_c, sums[0], sums[1])
        for q in range(z.Q):
            for b in range(z.B):
                row = q * bj + b * z.JJ
                send[b, q, rp] = sums[row:row + z.JJ].astype(BF16)

    def features_legendre():
        def body(rp, _):
            legendre(rows_of(cstage, rp), rp, fsend)
            return 0

        lax.fori_loop(0, z.RP, body, 0, unroll=2)

    def tangent_legendre():
        def body(rp, _):
            damped = damp[...] * adj[rp]
            adj[rp] = damped
            legendre(dt_scale * damped, rp, tsend)
            return 0

        lax.fori_loop(0, z.RP, body, 0, unroll=2)

    def fourier(recv, q, table, scale, send):
        def convert(b, _):
            block = recv[b, q].astype(F32)
            for rp in range(z.RP):
                row = pl.multiple_of((b * z.RP + rp) * z.PITCH, 8)
                fs[pl.ds(row, z.JJ), :] = block[rp]
            return 0

        lax.fori_loop(0, z.B, convert, 0)

        def group(g, _):
            parts = []
            for i in range(z.G):
                at = fs[pl.ds(g * z.G + i, z.RT, stride=z.PITCH), :].T.astype(BF16)
                parts.append(jnp.concatenate(
                    [at[c * z.VL:(c + 1) * z.VL] for c in range(4)], axis=1))
            y = dot(jnp.concatenate(parts, axis=0), table[...])
            if scale is not None:
                y = y * scale
            y = y.astype(BF16)
            for v in range(z.LV):
                for i in range(z.G):
                    send[v, q, g * z.G + i] = y[i * z.VL:(i + 1) * z.VL, v * z.O:(v + 1) * z.O]
            return 0

        lax.fori_loop(0, z.JJ // z.G, group, 0)

    def adjoint_fourier(q):
        def group(g, _):
            x = jnp.concatenate([
                jnp.concatenate([lg_recv[v, q, g * z.G + i] for v in range(z.LV)], axis=1)
                for i in range(z.G)], axis=0)
            y = dot_nt(x, tab_w[...])
            for i in range(z.G):
                yi = y[i * z.VL:(i + 1) * z.VL]
                st = jnp.concatenate([yi[:, c * z.RT:(c + 1) * z.RT] for c in range(4)], axis=0)
                fs2[pl.ds(g * z.G + i, z.RT, stride=z.PITCH), :] = st.T
            return 0

        lax.fori_loop(0, z.JJ // z.G, group, 0)

        def convert(b, _):
            for rp in range(z.RP):
                row = pl.multiple_of((b * z.RP + rp) * z.PITCH, 8)
                bsend[b, q, rp] = fs2[pl.ds(row, z.JJ), :].astype(BF16)
            return 0

        lax.fori_loop(0, z.B, convert, 0)

    def adjoint_legendre(q):
        def body(rp, _):
            b_t = jnp.concatenate(
                [brecv[b, q, rp].astype(F32) for b in range(z.B)], axis=0).T.astype(BF16)
            for r2 in range(2):
                rows = slice(r2 * half_c, (r2 + 1) * half_c)
                grad = dot(b_t[rows], tab[2 * rp + r2, q])
                adj[rp, rows] = adj[rp, rows] + jnp.where(upper(rp, r2), grad, 0.0)
            return 0

        lax.fori_loop(0, z.RP, body, 0, unroll=2)

    def observations(k):
        weights = [jnp.where(obs_time[i] == k, 1.0, 0.0).astype(F32) for i in range(z.NO)]

        def body(f, _):
            v, rest = f // z.LV // z.L, lax.rem(f, z.LV * z.L)
            row = (rest // z.L) * z.VL + v * z.L + lax.rem(rest, z.L)
            total = weights[0] * obs_all[0, f]
            for i in range(1, z.NO):
                total = total + weights[i] * obs_all[i, f]
            obs_s[pl.ds(row, z.J, stride=z.OPITCH), :] = total
            return 0

        lax.fori_loop(0, z.F, body, 0, unroll=4)

    ng = min(4, z.JJ)

    def network(q):
        def group(g, _):
            def columns(ref):
                return jnp.concatenate([
                    jnp.concatenate([ref[v, q, g * ng + i] for v in range(z.LV)], axis=0)
                    for i in range(ng)], axis=1)

            x = columns(lf_recv)
            t = columns(lt_recv)
            grad = None
            for h in range(0, z.H, z.HC):
                rows = slice(h, h + z.HC)
                b = bias[rows]
                pre = dot(w_in_t[rows], x) + jnp.concatenate([b] * ng, axis=1)
                logistic = 0.5 * jnp.tanh(0.5 * pre) + 0.5
                hid = pre * logistic
                pg = dot(w_out[rows], t) * (logistic + hid * (1.0 - logistic))
                low = pg.astype(BF16)
                acc_out[rows] += dot_nt(hid.astype(BF16), t)
                acc_in[rows] += dot_nt(low, x)
                total = pg[:, :z.O]
                for i in range(1, ng):
                    total = total + pg[:, i * z.O:(i + 1) * z.O]
                acc_b[rows] += total
                part = dot(w_in[:, rows], low)
                grad = part if grad is None else grad + part
            for i in range(ng):
                j = q * z.JJ + g * ng + i
                row = pl.multiple_of(j * z.OPITCH, 8)
                col = grad[:, i * z.O:(i + 1) * z.O] + obs_s[pl.ds(row, z.F), :]
                col = col.astype(BF16)
                for v in range(z.LV):
                    lg_send[v, q, g * ng + i] = col[v * z.VL:(v + 1) * z.VL]
            return 0

        lax.fori_loop(0, z.JJ // ng, group, 0)

    def to_device(src, dst, ssem, rsem, d):
        return pltpu.make_async_remote_copy(
            src_ref=src, dst_ref=dst, send_sem=ssem, recv_sem=rsem,
            device_id=(d // z.LV, lax.rem(d, z.LV)), device_id_type=MESH,
        )

    def reduce_send():
        for i, acc in enumerate((acc_in, acc_out, acc_b)):
            for d in range(z.ND):
                rs_send[d, i] = acc[d * z.HD:(d + 1) * z.HD].astype(BF16)
        rs_recv[me] = rs_send[me]
        others(z.ND, me, lambda d: to_device(
            rs_send.at[d], rs_recv.at[me], rs_s.at[d], rs_r.at[me], d).start())

    def gather_send():
        others(z.ND, me, lambda d: to_device(
            rs_send.at[d], rs_recv.at[d], rs_s.at[d], rs_r.at[d], d).wait())
        total = rs_recv[0].astype(F32)
        for d in range(1, z.ND):
            total = total + rs_recv[d].astype(F32)
        total = total.astype(BF16)
        ag_send[...] = total
        ag_recv[me] = total
        others(z.ND, me, lambda d: to_device(
            ag_send, ag_recv.at[me], ag_s.at[d], ag_r.at[me], d).start())

    def gather_wait():
        others(z.ND, me, lambda d: to_device(
            ag_send, ag_recv.at[d], ag_s.at[d], ag_r.at[d], d).wait())

    acc_in[...] = jnp.zeros_like(acc_in)
    acc_out[...] = jnp.zeros_like(acc_out)
    acc_b[...] = jnp.zeros_like(acc_b)

    for h in range(halves):
        ck_copy(z.S - 1, h).wait()
    for c in leg_copies:
        c.wait()
    features_legendre()
    feat_send((z.S - 1) % 2)
    if z.S > 1:
        for h in range(halves):
            ck_copy(z.S - 2, h).start()
    for h in range(halves):
        fc_copy(h).wait()

    def initial(rp, _):
        adj[rp] = rows_of(ostage, rp)
        return 0

    lax.fori_loop(0, z.RP, initial, 0)

    tang = (tsend, trecv, t_s, t_r)
    back = (bsend, brecv, b_s, b_r)
    lt = (lt_send, lt_recv, lt_s, lt_r)
    lf = (lf_send, lf_recv, lf_s, lf_r)
    lg = (lg_send, lg_recv, lg_s, lg_r)

    def step(i, _):
        k = z.S - 1 - i
        par = lax.rem(k, 2)
        tangent_legendre()
        for q in range(z.Q):
            band_send(*tang, q)
        feat_wait_recv(par)
        for q in range(z.Q):
            fourier(frecv.at[par], q, tab_w, None, lf_send)
            lev_send(*lf, q)

        @pl.when(k > 0)
        def _():
            for h in range(halves):
                ck_copy(k - 1, h).wait()
            feat_wait_send()
            features_legendre()
            feat_send(1 - par)

        @pl.when(k > 1)
        def _():
            for h in range(halves):
                ck_copy(k - 2, h).start()

        @pl.when(i == 0)
        def _():
            obs_copy.wait()

        observations(k)

        def do_t(q):
            band_wait_recv(*tang, q)
            fourier(trecv, q, tab_t, 1.0 / (z.O * z.LV), lt_send)
            lev_send(*lt, q)

        def do_n(q):
            lev_wait_recv(*lf, q)
            lev_wait_recv(*lt, q)
            network(q)
            lev_send(*lg, q)

        def do_b(q):
            lev_wait_recv(*lg, q)

            @pl.when(i > 0)
            def _():
                band_wait_send(*back, q)

            adjoint_fourier(q)
            band_send(*back, q)

        do_t(0)
        do_n(0)
        for q in range(1, z.Q):
            do_t(q)
            do_b(q - 1)
            do_n(q)

        @pl.when(k == 0)
        def _():
            reduce_send()

        do_b(z.Q - 1)

        @pl.when(k == 0)
        def _():
            gather_send()

        for q in range(z.Q):
            band_wait_recv(*back, q)
            adjoint_legendre(q)
        for q in range(z.Q):
            band_wait_send(*tang, q)
            lev_wait_send(*lf, q)
            lev_wait_send(*lt, q)
            lev_wait_send(*lg, q)
        return 0

    lax.fori_loop(0, z.S, step, 0)

    def final(rp, _):
        for r2 in range(2):
            for p in range(2):
                start = p * z.R + 2 * rp + r2
                c = r2 * half_c + p * z.VL
                for h in range(halves):
                    ostage[h, pl.ds(start, z.VL, stride=2 * z.R), :] = (
                        adj[rp, c:c + z.VL, h * LANES:(h + 1) * LANES])
        return 0

    lax.fori_loop(0, z.RP, final, 0)
    for h in range(halves):
        out_copy(h).start()
    gather_wait()
    gather_copy = pltpu.make_async_copy(ag_recv, gout, g_sem.at[0])
    gather_copy.start()
    feat_wait_send()
    for q in range(z.Q):
        band_wait_send(*back, q)
    for h in range(halves):
        out_copy(h).wait()
    gather_copy.wait()


def shards(checkpoints, final_cot, obs_cot, obs_time, wave_order, legendre, w_in, w_out, bias):
    local_waves, lat_count, wave_count = legendre.shape
    fields, levels = final_cot.shape[:2]
    z = Sizes(
        lax.axis_size("band"), lax.axis_size("lev"), checkpoints.shape[0], fields, levels,
        local_waves, wave_count, obs_cot.shape[3], obs_cot.shape[4], obs_cot.shape[0],
        w_in.shape[1])
    lon_count = z.O * z.LV
    order = wave_order.reshape(z.RT, 2).T[:, None, :, None]
    longitude = jnp.arange(lon_count, dtype=jnp.int32)
    phase = (order * longitude) % lon_count
    angles = 2.0 * jnp.pi / lon_count * phase.astype(F32)
    table = jnp.concatenate(
        [jnp.cos(angles).astype(BF16), -jnp.sin(angles).astype(BF16)], axis=1)
    weight = jnp.where(order == 0, 1.0, 2.0).astype(BF16)
    tab_w = (table * weight).reshape(4 * z.RT, lon_count)
    tab_t = table.reshape(4 * z.RT, lon_count)
    degree = jnp.arange(wave_count, dtype=jnp.int32).astype(F32)
    damp = (1.0 / (1.0 + 2.0 * degree * (degree + 1.0) / (wave_count * wave_count)))[None]

    def to_wire(w, axis):
        shape = w.shape[:axis] + (fields, z.LV, levels) + w.shape[axis + 1:]
        return jnp.swapaxes(w.reshape(shape), axis, axis + 1).reshape(w.shape)

    def from_wire(w, axis):
        shape = w.shape[:axis] + (z.LV, fields, levels) + w.shape[axis + 1:]
        return jnp.swapaxes(w.reshape(shape), axis, axis + 1).reshape(w.shape)

    w_in_p = to_wire(w_in, 0)
    w_out_p = to_wire(w_out, 1)
    any_space = pl.BlockSpec(memory_space=pl.ANY)
    smem = pl.BlockSpec(memory_space=pltpu.SMEM)
    vmem = pl.BlockSpec(memory_space=pltpu.VMEM)
    dma = pltpu.SemaphoreType.DMA
    band_buf = pltpu.VMEM((z.B, z.Q, z.RP, z.JJ, z.C), BF16)
    lev_buf = pltpu.VMEM((z.LV, z.Q, z.JJ, z.VL, z.O), BF16)
    halves = z.N // LANES
    reduce_buf = pltpu.VMEM((z.ND, 3, z.HD, z.F), BF16)
    scratch = [
        pltpu.VMEM((z.R, z.Q, z.B * z.JJ, z.N), BF16),
        pltpu.VMEM((z.RP, z.C, z.N), F32),
        band_buf, band_buf, band_buf,
        pltpu.VMEM((2, z.B, z.Q, z.RP, z.JJ, z.C), BF16),
        band_buf, band_buf,
        lev_buf, lev_buf, lev_buf, lev_buf, lev_buf, lev_buf,
        pltpu.VMEM((z.RT * z.PITCH, z.C), F32),
        pltpu.VMEM((z.RT * z.PITCH, z.C), F32),
        pltpu.VMEM((halves, z.ROWS, LANES), F32),
        pltpu.VMEM((halves, z.ROWS, LANES), F32),
        pltpu.VMEM((z.NO, z.F, z.J, z.O), F32),
        pltpu.VMEM((z.J * z.OPITCH, z.O), F32),
        pltpu.VMEM((z.H, z.F), F32), pltpu.VMEM((z.H, z.F), F32), pltpu.VMEM((z.H, z.O), F32),
        reduce_buf, reduce_buf,
        pltpu.VMEM((3, z.HD, z.F), BF16), reduce_buf,
        dma((z.Q, z.B)), dma((z.Q, z.B)), dma((z.B,)), dma((2, z.B)), dma((z.Q, z.B)), dma((z.Q, z.B)),
        dma((z.Q, z.LV)), dma((z.Q, z.LV)), dma((z.Q, z.LV)), dma((z.Q, z.LV)),
        dma((z.Q, z.LV)), dma((z.Q, z.LV)),
        dma((z.ND,)), dma((z.ND,)), dma((z.ND,)), dma((z.ND,)),
        dma((halves,)), dma((halves,)), dma((1,)), dma((z.B * z.Q,)), dma((halves,)), dma((1,)),
    ]
    grad_state, grads = pl.pallas_call(
        functools.partial(kernel, z),
        out_shape=[
            jax.ShapeDtypeStruct((z.ROWS, z.N), F32),
            jax.ShapeDtypeStruct((z.ND, 3, z.HD, z.F), BF16),
        ],
        in_specs=[any_space] * 4 + [smem] * 2 + [vmem] * 7,
        out_specs=[any_space, any_space],
        scratch_shapes=scratch,
        compiler_params=pltpu.CompilerParams(
            has_side_effects=True, vmem_limit_bytes=60 * 1024 * 1024),
    )(
        checkpoints.reshape(z.S, z.ROWS, z.N),
        final_cot.reshape(z.ROWS, z.N),
        obs_cot.reshape(z.NO, z.F, z.J, z.O),
        legendre,
        obs_time, wave_order, damp, tab_t, tab_w,
        w_in_p.T, w_in_p, w_out_p,
        jnp.broadcast_to(bias[:, None], (z.H, z.O)),
    )
    grads = jnp.swapaxes(grads, 0, 1).astype(F32).reshape(3, z.H, z.F)
    return (
        grad_state.reshape(final_cot.shape),
        from_wire(grads[0].T, 0),
        from_wire(grads[1], 1),
        jnp.sum(grads[2], axis=1),
    )


def solution(mesh):
    placed = (
        P(None, None, "lev", None, "band", None),
        P(None, "lev", None, "band", None),
        P(None, None, None, "band", "lev"),
        P(),
        P(),
        P("band", None, None),
        P(),
        P(),
        P(),
    )
    return jax.shard_map(
        shards,
        mesh=mesh,
        in_specs=placed,
        out_specs=(P(None, "lev", None, "band", None), P(), P(), P()),
        check_vma=False,
    )
```

time: 938 us -> 367 us (0.39); the launches traced: 925 us -> 365 us
  Pallas kernels: 0 us -> 344 us
  local copies, waits for them, and re-layouts: 285 us -> 14.1 us
  waiting for transfers between devices: 204 us -> 0 us
  blocking collectives: 194 us -> 0 us
  matrix products: 134 us -> 0 us
  starting transfers between devices: 67.6 us -> 0 us
  other arithmetic: 28.2 us -> 7 us
  between operations: 12.3 us -> 0.77 us
    pallas_call x0 -> x1, Pallas kernels: none -> 344 us  [shards(): pl.pallas_call(functools.partial(kernel, z), out_shape=[jax.ShapeDtypeStr...]
    reshape x38 -> x4, local copies, waits for them, and re-layouts: 249 us -> 2.54 us  [the longest x2 1.67 us: to_wire(): return jnp.swapaxes(w.reshape(shape), axis, axis + 1).reshape(w.shape)]
    all_to_all x13 -> x0, waiting for transfers between devices: 204 us -> none  [the longest x4 111 us: to_columns(): rows = lax.all_to_all(sums, 'band', split_axis=0, concat_axis=0, tiled=True)]
    all_to_all x6 -> x0, blocking collectives: 137 us -> none  [the longest x2 56.8 us: shards(): back = lax.all_to_all(back, 'band', split_axis=0, concat_axis=0, tiled=True)]
    dot_general x38 -> x0, matrix products: 134 us -> none  [the longest x4 28.8 us: network_grads(): jnp.einsum('jho,jfo->hf', hidden, tangent, preferred_element_type=jnp.flo...]
    all_to_all x13 -> x0, starting transfers between devices: 67.6 us -> none  [the longest x5 30 us: to_columns(): cols = lax.all_to_all(grid, 'lev', split_axis=0, concat_axis=0, tiled=True)]
    all_gather x1 -> x0, blocking collectives: 57.7 us -> none  [reduce_grads(): total = lax.all_gather(jnp.sum(parts, axis=0), axes, axis=0, tiled=True)]
    add x3 -> x0, other arithmetic: 12.9 us -> none  [the longest x2 12.2 us: shards(): sum((jnp.where(obs_time[i] == step, obs_cot[i], 0.0) for i in range(obs_c...]
  transfers between devices with their start and end apart: 13 -> 0, of which waited for: 10 -> 0; matrix products, arithmetic and copies ran while one was open for 19% -> 0% of each run, Pallas kernels for 0% -> 0%
where the time goes in v1:
time: 367 us; the launch traced here: 365 us
  Pallas kernels  344 us (94%)
  local copies, waits for them, and re-layouts  14.1 us (4%)
  other arithmetic  7 us (2%)
    pallas_call x1, Pallas kernels, shards(): pl.pallas_call(functools.partial(kernel, z), out_shape=[jax.ShapeDtypeStr...  344 us

profile of v1, /device:TPU:1, one launch (start us, length us, event | category | flops | bytes accessed | tf_op | source)
XLA Modules:
  0.0 365.4 jit_solution(16832226282388718794)
XLA Ops:
  0.6 0.0 copy-start.2
  0.6 0.6 add_divide_fusion.damp
  1.2 0.8 reshape.172
  2.0 0.1 copy.41
  2.1 0.9 copy.42
  3.1 0.0 copy-start.1
  3.1 0.8 copy.45.w_in_t
  3.8 1.0 copy.43
  4.9 0.8 copy.46.w_out
  5.6 2.1 fusion.6
  7.7 2.1 cosine_convert_fusion
  9.9 0.1 pad_maximum_fusion
  9.9 0.0 copy-start
  9.9 0.0 copy-done.2
  9.9 0.9 broadcast_in_dim.19.bias
  10.8 0.9 broadcast_multiply_fusion.tab_w
  11.7 0.0 copy-done.1
  11.7 0.0 copy-done
  11.7 343.6 %shard_map.120 = (f32[2048,256]{1,0:T(8,128)}, bf16[32,3,16,128]{3,2,1,0:T(8,128)(2,1)}) custom-call(f32[4,2048,256]{2,1,0:T(8,128)} %bitcast.34, f32[2048,256]{1,0:T(8,128)} %bitcast.38, f32[4,128,32,128]{3,2,1,0:T(8,128)} %bitcast.35, bf16[32,256,256]{2,1,0:T(8,128)(2,1)} %leg.1, s32[4]{0:T(128)} %obs_time.1, s32[256]{0:T(256)} %wave.1, ...), custom_call_target="tpu_custom_call" | custom-call | tf_op jit(solution)/shard_map/pallas_call | solution.py:533
  355.3 1.0 convert_bitcast_fusion
  356.4 0.1 slice_reduce_fusion
  356.5 0.7 reduce_sum.12
  357.2 0.1 copy.47
  357.3 0.7 copy.48
  358.0 1.8 copy.49
  359.9 1.6 reshape_squeeze.3
  361.4 0.8 copy.51
  362.3 3.2 copy.53
  (4 shorter events, 0.0 us)
Async XLA Ops:
  0.6 9.3 %copy-start.2 = (f32[512]{0:T(512)S(1)}, f32[512]{0:T(512)}, u32[]{:S(2)}) copy-start(f32[512]{0:T(512)} %param.17) | copy-start | bytes 6148
  3.1 8.7 %copy-start.1 = (bf16[4,4,8,512]{3,2,0,1:T(8,128)(2,1)}, bf16[4,4,8,512]{3,2,0,1:T(8,128)(2,1)S(1)}, u32[]{:S(2)}) copy-start(bf16[4,4,8,512]{3,2,0,1:T(8,128)(2,1)S(1)} %copy.42) | copy-start | bytes 393220
  9.9 1.8 copy-start

commit v2 on v1

--- a/solution.py
+++ b/solution.py
@@ -41,11 +41,16 @@
         self.ROWS = self.VL * 2 * waves
         self.G = min(8, self.JJ)
         self.HC = min(256, hidden)
+        self.joint = lat % (8 * levs) == 0 and self.RP % 4 == 0
+        if self.joint:
+            self.JD, self.JQ, self.RG = lat // levs, 4, 4
+            self.Q = self.JD // self.JQ
 
 
 def kernel(
-    z, ck, fc, obs, leg, obs_time, wave, damp, tab_t, tab_w, w_in_t, w_in, w_out, bias,
+    z, ck, fc, obs, leg, obs_time, wave, w_in_raw, w_out_raw, bias_raw,
     out, gout,
+    tab_t, tab_w, w_in_t, w_in, w_out, bias, orders, damp,
     tab, adj, tsend, trecv, fsend, frecv, bsend, brecv,
     lf_send, lf_recv, lt_send, lt_recv, lg_send, lg_recv,
     fs, fs2, cstage, ostage, obs_all, obs_s, acc_in, acc_out, acc_b,
@@ -71,10 +76,11 @@
 
     def others(count, own, body):
         def step(d, _):
-            body(lax.rem(own + d, count))
-            return 0
-
-        lax.fori_loop(1, count, step, 0)
+            off = d + 1
+            body(lax.rem(own + off, count))
+            return 0
+
+        lax.fori_loop(0, count - 1, step, 0)
 
     def band_send(send, recv, ssem, rsem, q):
         others(z.B, me_b, lambda b: to_band(
@@ -89,18 +95,19 @@
         others(z.B, me_b, lambda b: to_band(
             send.at[b, q], recv.at[b, q], ssem.at[q, b], rsem.at[q, b], b).wait_send())
 
-    def feat_send(par):
+    def feat_send(par, q):
         others(z.B, me_b, lambda b: to_band(
-            fsend.at[b], frecv.at[par, me_b], f_s.at[b], f_r.at[par, me_b], b).start())
-        frecv[par, me_b] = fsend[me_b]
-
-    def feat_wait_recv(par):
+            fsend.at[b, q], frecv.at[par, me_b, q], f_s.at[q, b], f_r.at[par, q, me_b], b).start())
+        frecv[par, me_b, q] = fsend[me_b, q]
+
+    def feat_wait_recv(par, q):
         others(z.B, me_b, lambda b: to_band(
-            fsend.at[b], frecv.at[par, b], f_s.at[b], f_r.at[par, b], b).wait_recv())
+            fsend.at[b, q], frecv.at[par, b, q], f_s.at[q, b], f_r.at[par, q, b], b).wait_recv())
 
     def feat_wait_send():
-        others(z.B, me_b, lambda b: to_band(
-            fsend.at[b], frecv.at[0, b], f_s.at[b], f_r.at[0, b], b).wait_send())
+        for q in range(z.Q):
+            others(z.B, me_b, lambda b: to_band(
+                fsend.at[b, q], frecv.at[0, b, q], f_s.at[q, b], f_r.at[0, q, b], b).wait_send())
 
     def lev_send(send, recv, ssem, rsem, q):
         others(z.LV, me_l, lambda v: to_lev(
@@ -122,10 +129,6 @@
     def fc_copy(h):
         return pltpu.make_async_copy(
             fc.at[:, pl.ds(h * LANES, LANES)], ostage.at[h], fc_sem.at[h])
-
-    def out_copy(h):
-        return pltpu.make_async_copy(
-            ostage.at[h], out.at[:, pl.ds(h * LANES, LANES)], out_sem.at[h])
 
     halves = z.N // LANES
     bj = z.B * z.JJ
@@ -308,6 +311,40 @@
 
         lax.fori_loop(0, z.JJ // ng, group, 0)
 
+    def prepare():
+        def wire(w):
+            return jnp.concatenate([
+                w[(v * z.LV + l) * z.L:(v * z.LV + l + 1) * z.L]
+                for l in range(z.LV) for v in range(z.V)], axis=0)
+
+        wi = wire(w_in_raw[...].astype(F32))
+        w_in[...] = wi.astype(BF16)
+        w_in_t[...] = wi.T.astype(BF16)
+        w_out[...] = wire(w_out_raw[...].astype(F32).T).T.astype(BF16)
+        bias[...] = jnp.broadcast_to(bias_raw[...], (z.O, z.H)).T
+
+        def fill(i, _):
+            for r2 in range(2):
+                orders[pl.ds(r2 * z.RT + i, 1), :] = jnp.full((1, LANES), wave[2 * i + r2], jnp.int32)
+            return 0
+
+        lax.fori_loop(0, z.RT, fill, 0, unroll=4)
+        lon = z.O * z.LV
+        for r2 in range(2):
+            order = orders[r2 * z.RT:(r2 + 1) * z.RT]
+            weight = jnp.where(order == 0, 1.0, 2.0).astype(F32)
+            for tile in range(lon // LANES):
+                cols = slice(tile * LANES, (tile + 1) * LANES)
+                longitude = lax.broadcasted_iota(jnp.int32, (z.RT, LANES), 1) + tile * LANES
+                turn = (order * longitude).astype(F32)
+                turn = turn - jnp.floor(turn * (1.0 / lon)) * lon
+                angle = (2.0 * jnp.pi / lon) * turn
+                for p, value in enumerate((jnp.cos(angle), -jnp.sin(angle))):
+                    rows = slice((2 * r2 + p) * z.RT, (2 * r2 + p + 1) * z.RT)
+                    value = value.astype(BF16)
+                    tab_t[rows, cols] = value
+                    tab_w[rows, cols] = (value.astype(F32) * weight).astype(BF16)
+
     def to_device(src, dst, ssem, rsem, d):
         return pltpu.make_async_remote_copy(
             src_ref=src, dst_ref=dst, send_sem=ssem, recv_sem=rsem,
@@ -338,19 +375,17 @@
         others(z.ND, me, lambda d: to_device(
             ag_send, ag_recv.at[d], ag_s.at[d], ag_r.at[d], d).wait())
 
-    acc_in[...] = jnp.zeros_like(acc_in)
-    acc_out[...] = jnp.zeros_like(acc_out)
-    acc_b[...] = jnp.zeros_like(acc_b)
-
     for h in range(halves):
         ck_copy(z.S - 1, h).wait()
     for c in leg_copies:
         c.wait()
     features_legendre()
-    feat_send((z.S - 1) % 2)
+    feat_send((z.S - 1) % 2, 0)
     if z.S > 1:
         for h in range(halves):
             ck_copy(z.S - 2, h).start()
+    degrees = lax.broadcasted_iota(jnp.int32, (1, z.N), 1).astype(F32)
+    damp[...] = 1.0 / (1.0 + 2.0 * degrees * (degrees + 1.0) / (z.N * z.N))
     for h in range(halves):
         fc_copy(h).wait()
 
@@ -366,35 +401,25 @@
     lf = (lf_send, lf_recv, lf_s, lf_r)
     lg = (lg_send, lg_recv, lg_s, lg_r)
 
+    tangent_legendre()
+    for q in range(z.Q):
+        if q > 0:
+            feat_send((z.S - 1) % 2, q)
+        band_send(*tang, q)
+    acc_in[...] = jnp.zeros_like(acc_in)
+    acc_out[...] = jnp.zeros_like(acc_out)
+    acc_b[...] = jnp.zeros_like(acc_b)
+    prepare()
+    obs_copy.wait()
+
     def step(i, _):
         k = z.S - 1 - i
         par = lax.rem(k, 2)
-        tangent_legendre()
-        for q in range(z.Q):
-            band_send(*tang, q)
-        feat_wait_recv(par)
-        for q in range(z.Q):
+
+        def do_f(q):
+            feat_wait_recv(par, q)
             fourier(frecv.at[par], q, tab_w, None, lf_send)
             lev_send(*lf, q)
-
-        @pl.when(k > 0)
-        def _():
-            for h in range(halves):
-                ck_copy(k - 1, h).wait()
-            feat_wait_send()
-            features_legendre()
-            feat_send(1 - par)
-
-        @pl.when(k > 1)
-        def _():
-            for h in range(halves):
-                ck_copy(k - 2, h).start()
-
-        @pl.when(i == 0)
-        def _():
-            obs_copy.wait()
-
-        observations(k)
 
         def do_t(q):
             band_wait_recv(*tang, q)
@@ -417,7 +442,25 @@
             adjoint_fourier(q)
             band_send(*back, q)
 
+        do_f(0)
+
+        @pl.when(k > 0)
+        def _():
+            for h in range(halves):
+                ck_copy(k - 1, h).wait()
+            feat_wait_send()
+            features_legendre()
+            feat_send(1 - par, 0)
+
+        @pl.when(k > 1)
+        def _():
+            for h in range(halves):
+                ck_copy(k - 2, h).start()
+
+        observations(k)
         do_t(0)
+        for q in range(1, z.Q):
+            do_f(q)
         do_n(0)
         for q in range(1, z.Q):
             do_t(q)
@@ -430,6 +473,11 @@
 
         do_b(z.Q - 1)
 
+        @pl.when(k > 0)
+        def _():
+            for q in range(1, z.Q):
+                feat_send(1 - par, q)
+
         @pl.when(k == 0)
         def _():
             gather_send()
@@ -439,35 +487,475 @@
             adjoint_legendre(q)
         for q in range(z.Q):
             band_wait_send(*tang, q)
+
+        @pl.when(k > 0)
+        def _():
+            tangent_legendre()
+            for q in range(z.Q):
+                band_send(*tang, q)
+
+        for q in range(z.Q):
             lev_wait_send(*lf, q)
             lev_wait_send(*lt, q)
             lev_wait_send(*lg, q)
         return 0
 
     lax.fori_loop(0, z.S, step, 0)
-
-    def final(rp, _):
-        for r2 in range(2):
-            for p in range(2):
-                start = p * z.R + 2 * rp + r2
-                c = r2 * half_c + p * z.VL
-                for h in range(halves):
-                    ostage[h, pl.ds(start, z.VL, stride=2 * z.R), :] = (
-                        adj[rp, c:c + z.VL, h * LANES:(h + 1) * LANES])
-        return 0
-
-    lax.fori_loop(0, z.RP, final, 0)
-    for h in range(halves):
-        out_copy(h).start()
+    adj_copy = pltpu.make_async_copy(adj, out, out_sem.at[0])
+    adj_copy.start()
     gather_wait()
     gather_copy = pltpu.make_async_copy(ag_recv, gout, g_sem.at[0])
     gather_copy.start()
     feat_wait_send()
     for q in range(z.Q):
         band_wait_send(*back, q)
+    adj_copy.wait()
+    gather_copy.wait()
+
+
+def joint_kernel(
+    z, ck, fc, obs, leg, obs_time, wave, w_in_raw, w_out_raw, bias_raw,
+    out, gout,
+    tab_t, tab_w, w_in_t, w_in, w_out, bias, orders, damp,
+    tab, adj, tsend, trecv, fsend, frecv, bsend, brecv, osend, orecv,
+    feats, tangs, fs, fs2, cstage, ostage, obs_all, obs_s, acc_in, acc_out, acc_b,
+    rs_send, rs_recv, ag_send, ag_recv,
+    t_s, t_r, f_s, f_r, b_s, b_r, o_s, o_r, rs_s, rs_r, ag_s, ag_r,
+    ck_sem, fc_sem, obs_sem, leg_sem, out_sem, g_sem,
+):
+    me_b = lax.axis_index("band")
+    me_l = lax.axis_index("lev")
+    me = me_b * z.LV + me_l
+    halves = z.N // LANES
+    lon = z.O * z.LV
+    half_c = 2 * z.VL
+
+    def others(count, own, body):
+        def step(d, _):
+            body(lax.rem(own + d, count))
+            return 0
+
+        lax.fori_loop(1, count, step, 0)
+
+    def remote(src, dst, ssem, rsem, d):
+        return pltpu.make_async_remote_copy(
+            src_ref=src, dst_ref=dst, send_sem=ssem, recv_sem=rsem,
+            device_id=(d // z.LV, lax.rem(d, z.LV)), device_id_type=MESH,
+        )
+
+    def send_all(send, recv, ssem, rsem, q):
+        others(z.ND, me, lambda d: remote(
+            send.at[d, q], recv.at[me, q], ssem.at[q, d], rsem.at[q, me], d).start())
+        recv[me, q] = send[me, q]
+
+    def wait_recv(send, recv, ssem, rsem, q):
+        others(z.ND, me, lambda d: remote(
+            send.at[d, q], recv.at[d, q], ssem.at[q, d], rsem.at[q, d], d).wait_recv())
+
+    def wait_send(send, recv, ssem, rsem, q):
+        others(z.ND, me, lambda d: remote(
+            send.at[d, q], recv.at[d, q], ssem.at[q, d], rsem.at[q, d], d).wait_send())
+
+    def obs_send(par):
+        others(z.LV, me_l, lambda v: remote(
+            osend.at[v], orecv.at[par, me_l], o_s.at[v], o_r.at[par, me_l],
+            me_b * z.LV + v).start())
+        orecv[par, me_l] = osend[me_l]
+
+    def obs_wait_recv(par):
+        others(z.LV, me_l, lambda v: remote(
+            osend.at[v], orecv.at[par, v], o_s.at[v], o_r.at[par, v],
+            me_b * z.LV + v).wait_recv())
+
+    def obs_wait_send():
+        others(z.LV, me_l, lambda v: remote(
+            osend.at[v], orecv.at[0, v], o_s.at[v], o_r.at[0, v],
+            me_b * z.LV + v).wait_send())
+
+    def ck_copy(k, h):
+        return pltpu.make_async_copy(
+            ck.at[k, :, pl.ds(h * LANES, LANES)], cstage.at[h], ck_sem.at[h])
+
+    def fc_copy(h):
+        return pltpu.make_async_copy(
+            fc.at[:, pl.ds(h * LANES, LANES)], ostage.at[h], fc_sem.at[h])
+
+    leg_copy = pltpu.make_async_copy(leg, tab, leg_sem.at[0])
+    obs_copy = pltpu.make_async_copy(obs, obs_all, obs_sem.at[0])
     for h in range(halves):
-        out_copy(h).wait()
+        ck_copy(z.S - 1, h).start()
+    leg_copy.start()
+    for h in range(halves):
+        fc_copy(h).start()
+    obs_copy.start()
+
+    degree = lax.broadcasted_iota(jnp.int32, (half_c, z.N), 1)
+
+    def upper(rp, r2):
+        return degree >= wave[me_b * z.R + 2 * rp + r2]
+
+    def rows_of(stage, rp):
+        parts = []
+        for r2 in range(2):
+            for p in range(2):
+                start = p * z.R + 2 * rp + r2
+                parts.append(jnp.concatenate(
+                    [stage[h, pl.ds(start, z.VL, stride=2 * z.R), :] for h in range(halves)], axis=1))
+        return jnp.concatenate(parts, axis=0)
+
+    lat = z.ND * z.JD
+    lane = lax.broadcasted_iota(jnp.int32, (lat, z.C), 1)
+
+    def legendre(s, rp):
+        masked = jnp.concatenate(
+            [jnp.where(upper(rp, r2), s[r2 * half_c:(r2 + 1) * half_c], 0.0) for r2 in range(2)],
+            axis=0).astype(BF16)
+        sums = [dot_nt(tab[2 * rp + r2], masked) for r2 in range(2)]
+        return jnp.where(lane < half_c, sums[0], sums[1]).reshape(z.ND, z.JD, z.C)
+
+    def legendre_groups(spectral, send):
+        def body(g, _):
+            sums = [legendre(spectral(g * z.RG + i), g * z.RG + i) for i in range(z.RG)]
+            row = pl.multiple_of(g * z.RG * z.JQ, z.RG * z.JQ)
+            for q in range(z.Q):
+                block = jnp.concatenate(
+                    [s[:, q * z.JQ:(q + 1) * z.JQ] for s in sums], axis=1)
+                send[:, q, pl.ds(row, z.RG * z.JQ), :] = block.astype(BF16)
+            return 0
+
+        lax.fori_loop(0, z.RP // z.RG, body, 0)
+
+    def features_legendre():
+        legendre_groups(lambda rp: rows_of(cstage, rp), fsend)
+
+    def tangent_legendre():
+        def damped(rp):
+            value = damp[...] * adj[rp]
+            adj[rp] = value
+            return dt_scale * value
+
+        legendre_groups(damped, tsend)
+
+    block = z.RP * z.JQ
+
+    def fourier(recv, q, table, scale, dst):
+        def convert(b, _):
+            for v in range(z.LV):
+                row = pl.multiple_of((v * z.B + b) * block, block)
+                fs[pl.ds(row, block), :] = recv[b * z.LV + v, q].astype(F32)
+            return 0
+
+        lax.fori_loop(0, z.B, convert, 0, unroll=2)
+        parts = []
+        for i in range(z.JQ):
+            for v in range(z.LV):
+                at = fs[pl.ds(v * z.B * block + i, z.RT, stride=z.JQ), :].T.astype(BF16)
+                parts.append(jnp.concatenate(
+                    [at[c * z.VL:(c + 1) * z.VL] for c in range(4)], axis=1))
+        y = dot(jnp.concatenate(parts, axis=0), table[...])
+        if scale is not None:
+            y = y * scale
+        y = y.astype(BF16)
+        for i in range(z.JQ):
+            dst[q * z.JQ + i] = y[i * z.F:(i + 1) * z.F]
+
+    def network(q, par):
+        def column(i, _):
+            j = q * z.JQ + i
+            x = feats[j]
+            t = tangs[j]
+            grad = None
+            for h in range(0, z.H, z.HC):
+                rows = slice(h, h + z.HC)
+                pre = dot(w_in_t[rows], x) + jnp.concatenate([bias[rows]] * z.LV, axis=1)
+                logistic = 0.5 * jnp.tanh(0.5 * pre) + 0.5
+                hid = pre * logistic
+                pg = dot(w_out[rows], t) * (logistic + hid * (1.0 - logistic))
+                low = pg.astype(BF16)
+                acc_out[rows] += dot_nt(hid.astype(BF16), t)
+                acc_in[rows] += dot_nt(low, x)
+                total = pg[:, :z.O]
+                for v in range(1, z.LV):
+                    total = total + pg[:, v * z.O:(v + 1) * z.O]
+                acc_b[rows] += total
+                part = dot(w_in[:, rows], low)
+                grad = part if grad is None else grad + part
+            grad = grad + jnp.concatenate(
+                [orecv[par, v, j].astype(F32) for v in range(z.LV)], axis=1)
+            y = dot_nt(grad.astype(BF16), tab_w[...])
+            for v in range(z.LV):
+                yv = y[v * z.VL:(v + 1) * z.VL]
+                st = jnp.concatenate([yv[:, c * z.RT:(c + 1) * z.RT] for c in range(4)], axis=0)
+                fs2[pl.ds(v * z.B * block + i, z.RT, stride=z.JQ), :] = st.T
+            return 0
+
+        lax.fori_loop(0, z.JQ, column, 0)
+
+        def convert(b, _):
+            for v in range(z.LV):
+                row = pl.multiple_of((v * z.B + b) * block, block)
+                bsend[b * z.LV + v, q] = fs2[pl.ds(row, block), :].astype(BF16)
+            return 0
+
+        lax.fori_loop(0, z.B, convert, 0, unroll=2)
+
+    def adjoint_legendre():
+        def body(g, _):
+            row = pl.multiple_of(g * z.RG * z.JQ, z.RG * z.JQ)
+            chunks = [brecv[:, q, pl.ds(row, z.RG * z.JQ), :].astype(F32) for q in range(z.Q)]
+            for i in range(z.RG):
+                rp = g * z.RG + i
+                b_t = jnp.concatenate(
+                    [c[:, i * z.JQ:(i + 1) * z.JQ] for c in chunks],
+                    axis=1).reshape(lat, z.C).T.astype(BF16)
+                for r2 in range(2):
+                    rows = slice(r2 * half_c, (r2 + 1) * half_c)
+                    grad = dot(b_t[rows], tab[2 * rp + r2])
+                    adj[rp, rows] = adj[rp, rows] + jnp.where(upper(rp, r2), grad, 0.0)
+            return 0
+
+        lax.fori_loop(0, z.RP // z.RG, body, 0)
+
+    def observations(k):
+        weights = [jnp.where(obs_time[i] == k, 1.0, 0.0).astype(F32) for i in range(z.NO)]
+
+        def body(f, _):
+            v, rest = f // z.LV // z.L, lax.rem(f, z.LV * z.L)
+            row = (rest // z.L) * z.VL + v * z.L + lax.rem(rest, z.L)
+            total = weights[0] * obs_all[0, f]
+            for i in range(1, z.NO):
+                total = total + weights[i] * obs_all[i, f]
+            obs_s[pl.ds(row, z.J, stride=z.OPITCH), :] = total
+            return 0
+
+        lax.fori_loop(0, z.F, body, 0, unroll=4)
+
+        def pack(v, _):
+            for j in range(z.JD):
+                row = pl.multiple_of((v * z.JD + j) * z.OPITCH, 8)
+                osend[v, j] = obs_s[pl.ds(row, z.F), :].astype(BF16)
+            return 0
+
+        lax.fori_loop(0, z.LV, pack, 0)
+
+    def prepare():
+        def wire(w):
+            return jnp.concatenate([
+                w[(v * z.LV + l) * z.L:(v * z.LV + l + 1) * z.L]
+                for l in range(z.LV) for v in range(z.V)], axis=0)
+
+        wi = wire(w_in_raw[...].astype(F32))
+        w_in[...] = wi.astype(BF16)
+        w_in_t[...] = wi.T.astype(BF16)
+        w_out[...] = wire(w_out_raw[...].astype(F32).T).T.astype(BF16)
+        bias[...] = jnp.broadcast_to(bias_raw[...], (z.O, z.H)).T
+
+        def fill(i, _):
+            for r2 in range(2):
+                orders[pl.ds(r2 * z.RT + i, 1), :] = jnp.full((1, LANES), wave[2 * i + r2], jnp.int32)
+            return 0
+
+        lax.fori_loop(0, z.RT, fill, 0, unroll=4)
+        for r2 in range(2):
+            order = orders[r2 * z.RT:(r2 + 1) * z.RT]
+            weight = jnp.where(order == 0, 1.0, 2.0).astype(F32)
+            for tile in range(lon // LANES):
+                cols = slice(tile * LANES, (tile + 1) * LANES)
+                longitude = lax.broadcasted_iota(jnp.int32, (z.RT, LANES), 1) + tile * LANES
+                turn = (order * longitude).astype(F32)
+                turn = turn - jnp.floor(turn * (1.0 / lon)) * lon
+                angle = (2.0 * jnp.pi / lon) * turn
+                for p, value in enumerate((jnp.cos(angle), -jnp.sin(angle))):
+                    rows = slice((2 * r2 + p) * z.RT, (2 * r2 + p + 1) * z.RT)
+                    value = value.astype(BF16)
+                    tab_t[rows, cols] = value
+                    tab_w[rows, cols] = (value.astype(F32) * weight).astype(BF16)
+
+    def reduce_send():
+        for i, acc in enumerate((acc_in, acc_out, acc_b)):
+            for d in range(z.ND):
+                rs_send[d, i] = acc[d * z.HD:(d + 1) * z.HD].astype(BF16)
+        rs_recv[me] = rs_send[me]
+        others(z.ND, me, lambda d: remote(
+            rs_send.at[d], rs_recv.at[me], rs_s.at[d], rs_r.at[me], d).start())
+
+    def gather_send():
+        others(z.ND, me, lambda d: remote(
+            rs_send.at[d], rs_recv.at[d], rs_s.at[d], rs_r.at[d], d).wait())
+        total = rs_recv[0].astype(F32)
+        for d in range(1, z.ND):
+            total = total + rs_recv[d].astype(F32)
+        total = total.astype(BF16)
+        ag_send[...] = total
+        ag_recv[me] = total
+        others(z.ND, me, lambda d: remote(
+            ag_send, ag_recv.at[me], ag_s.at[d], ag_r.at[me], d).start())
+
+    def gather_wait():
+        others(z.ND, me, lambda d: remote(
+            ag_send, ag_recv.at[d], ag_s.at[d], ag_r.at[d], d).wait())
+
+    for h in range(halves):
+        ck_copy(z.S - 1, h).wait()
+    leg_copy.wait()
+    tang = (tsend, trecv, t_s, t_r)
+    back = (bsend, brecv, b_s, b_r)
+
+    def feat(par):
+        return (fsend, frecv.at[par], f_s, f_r.at[par])
+
+    features_legendre()
+    first = (z.S - 1) % 2
+    send_all(*feat(first), 0)
+    if z.S > 1:
+        for h in range(halves):
+            ck_copy(z.S - 2, h).start()
+    degrees = lax.broadcasted_iota(jnp.int32, (1, z.N), 1).astype(F32)
+    damp[...] = 1.0 / (1.0 + 2.0 * degrees * (degrees + 1.0) / (z.N * z.N))
+    for h in range(halves):
+        fc_copy(h).wait()
+
+    def initial(rp, _):
+        adj[rp] = rows_of(ostage, rp)
+        return 0
+
+    lax.fori_loop(0, z.RP, initial, 0)
+    tangent_legendre()
+    for q in range(z.Q):
+        if q > 0:
+            send_all(*feat(first), q)
+        send_all(*tang, q)
+    obs_copy.wait()
+    observations(z.S - 1)
+    obs_send(first)
+    acc_in[...] = jnp.zeros_like(acc_in)
+    acc_out[...] = jnp.zeros_like(acc_out)
+    acc_b[...] = jnp.zeros_like(acc_b)
+    prepare()
+
+    def step(i, _):
+        k = z.S - 1 - i
+        par = lax.rem(k, 2)
+
+        def do_f(q):
+            wait_recv(*feat(par), q)
+            fourier(frecv.at[par], q, tab_w, None, feats)
+
+        def do_n(q):
+            wait_recv(*tang, q)
+            fourier(trecv, q, tab_t, 1.0 / lon, tangs)
+            if q == 0:
+                obs_wait_recv(par)
+
+            @pl.when(i > 0)
+            def _():
+                wait_send(*back, q)
+
+            network(q, par)
+            send_all(*back, q)
+
+        do_f(0)
+
+        @pl.when(k > 0)
+        def _():
+            for h in range(halves):
+                ck_copy(k - 1, h).wait()
+            for q in range(z.Q):
+                wait_send(*feat(0), q)
+            features_legendre()
+            send_all(*feat(1 - par), 0)
+
+        @pl.when(k > 1)
+        def _():
+            for h in range(halves):
+                ck_copy(k - 2, h).start()
+
+        do_n(0)
+
+        @pl.when(k > 0)
+        def _():
+            obs_wait_send()
+            observations(k - 1)
+            obs_send(1 - par)
+
+        for q in range(1, z.Q):
+            do_f(q)
+            do_n(q)
+
+        @pl.when(k == 0)
+        def _():
+            reduce_send()
+
+        @pl.when(k > 0)
+        def _():
+            for q in range(1, z.Q):
+                send_all(*feat(1 - par), q)
+
+        @pl.when(k == 0)
+        def _():
+            gather_send()
+
+        for q in range(z.Q):
+            wait_recv(*back, q)
+        adjoint_legendre()
+        for q in range(z.Q):
+            wait_send(*tang, q)
+
+        @pl.when(k > 0)
+        def _():
+            tangent_legendre()
+            for q in range(z.Q):
+                send_all(*tang, q)
+
+        return 0
+
+    lax.fori_loop(0, z.S, step, 0)
+    adj_copy = pltpu.make_async_copy(adj, out, out_sem.at[0])
+    adj_copy.start()
+    gather_wait()
+    gather_copy = pltpu.make_async_copy(ag_recv, gout, g_sem.at[0])
+    gather_copy.start()
+    obs_wait_send()
+    for q in range(z.Q):
+        wait_send(*feat(0), q)
+        wait_send(*back, q)
+    adj_copy.wait()
     gather_copy.wait()
+
+
+def finish(z, adj, grads, out, grad_in, grad_out, grad_bias, stage, flat, sem):
+    half_c = 2 * z.VL
+    copies = []
+    for h in range(z.N // LANES):
+        cols = slice(h * LANES, (h + 1) * LANES)
+
+        def body(rp, _):
+            for r2 in range(2):
+                for p in range(2):
+                    start = p * z.R + 2 * rp + r2
+                    c = r2 * half_c + p * z.VL
+                    stage[h, pl.ds(start, z.VL, stride=2 * z.R), :] = adj[rp, c:c + z.VL, cols]
+            return 0
+
+        lax.fori_loop(0, z.RP, body, 0)
+        copy = pltpu.make_async_copy(stage.at[h], out.at[:, pl.ds(h * LANES, LANES)], sem.at[h])
+        copy.start()
+        copies.append(copy)
+
+    for d in range(z.ND):
+        for i in range(3):
+            flat[i, d * z.HD:(d + 1) * z.HD] = grads[d, i].astype(F32)
+
+    def from_wire(w):
+        return jnp.concatenate([
+            w[(l * z.V + v) * z.L:(l * z.V + v + 1) * z.L]
+            for v in range(z.V) for l in range(z.LV)], axis=0)
+
+    grad_in[...] = from_wire(flat[0].T)
+    grad_out[...] = from_wire(flat[1].T).T
+    grad_bias[...] = jnp.sum(flat[2].T, axis=0, keepdims=True)
+    for copy in copies:
+        copy.wait()
 
 
 def shards(checkpoints, final_cot, obs_cot, obs_time, wave_order, legendre, w_in, w_out, bias):
@@ -477,46 +965,19 @@
         lax.axis_size("band"), lax.axis_size("lev"), checkpoints.shape[0], fields, levels,
         local_waves, wave_count, obs_cot.shape[3], obs_cot.shape[4], obs_cot.shape[0],
         w_in.shape[1])
-    lon_count = z.O * z.LV
-    order = wave_order.reshape(z.RT, 2).T[:, None, :, None]
-    longitude = jnp.arange(lon_count, dtype=jnp.int32)
-    phase = (order * longitude) % lon_count
-    angles = 2.0 * jnp.pi / lon_count * phase.astype(F32)
-    table = jnp.concatenate(
-        [jnp.cos(angles).astype(BF16), -jnp.sin(angles).astype(BF16)], axis=1)
-    weight = jnp.where(order == 0, 1.0, 2.0).astype(BF16)
-    tab_w = (table * weight).reshape(4 * z.RT, lon_count)
-    tab_t = table.reshape(4 * z.RT, lon_count)
-    degree = jnp.arange(wave_count, dtype=jnp.int32).astype(F32)
-    damp = (1.0 / (1.0 + 2.0 * degree * (degree + 1.0) / (wave_count * wave_count)))[None]
-
-    def to_wire(w, axis):
-        shape = w.shape[:axis] + (fields, z.LV, levels) + w.shape[axis + 1:]
-        return jnp.swapaxes(w.reshape(shape), axis, axis + 1).reshape(w.shape)
-
-    def from_wire(w, axis):
-        shape = w.shape[:axis] + (z.LV, fields, levels) + w.shape[axis + 1:]
-        return jnp.swapaxes(w.reshape(shape), axis, axis + 1).reshape(w.shape)
-
-    w_in_p = to_wire(w_in, 0)
-    w_out_p = to_wire(w_out, 1)
     any_space = pl.BlockSpec(memory_space=pl.ANY)
     smem = pl.BlockSpec(memory_space=pltpu.SMEM)
     vmem = pl.BlockSpec(memory_space=pltpu.VMEM)
     dma = pltpu.SemaphoreType.DMA
-    band_buf = pltpu.VMEM((z.B, z.Q, z.RP, z.JJ, z.C), BF16)
-    lev_buf = pltpu.VMEM((z.LV, z.Q, z.JJ, z.VL, z.O), BF16)
     halves = z.N // LANES
     reduce_buf = pltpu.VMEM((z.ND, 3, z.HD, z.F), BF16)
-    scratch = [
-        pltpu.VMEM((z.R, z.Q, z.B * z.JJ, z.N), BF16),
-        pltpu.VMEM((z.RP, z.C, z.N), F32),
-        band_buf, band_buf, band_buf,
-        pltpu.VMEM((2, z.B, z.Q, z.RP, z.JJ, z.C), BF16),
-        band_buf, band_buf,
-        lev_buf, lev_buf, lev_buf, lev_buf, lev_buf, lev_buf,
-        pltpu.VMEM((z.RT * z.PITCH, z.C), F32),
-        pltpu.VMEM((z.RT * z.PITCH, z.C), F32),
+    lon = z.O * z.LV
+    weights = [
+        pltpu.VMEM((4 * z.RT, lon), BF16), pltpu.VMEM((4 * z.RT, lon), BF16),
+        pltpu.VMEM((z.H, z.F), BF16), pltpu.VMEM((z.F, z.H), BF16), pltpu.VMEM((z.H, z.F), BF16),
+        pltpu.VMEM((z.H, z.O), F32), pltpu.VMEM((2 * z.RT, LANES), jnp.int32), pltpu.VMEM((1, z.N), F32),
+    ]
+    stages = [
         pltpu.VMEM((halves, z.ROWS, LANES), F32),
         pltpu.VMEM((halves, z.ROWS, LANES), F32),
         pltpu.VMEM((z.NO, z.F, z.J, z.O), F32),
@@ -524,19 +985,56 @@
         pltpu.VMEM((z.H, z.F), F32), pltpu.VMEM((z.H, z.F), F32), pltpu.VMEM((z.H, z.O), F32),
         reduce_buf, reduce_buf,
         pltpu.VMEM((3, z.HD, z.F), BF16), reduce_buf,
-        dma((z.Q, z.B)), dma((z.Q, z.B)), dma((z.B,)), dma((2, z.B)), dma((z.Q, z.B)), dma((z.Q, z.B)),
-        dma((z.Q, z.LV)), dma((z.Q, z.LV)), dma((z.Q, z.LV)), dma((z.Q, z.LV)),
-        dma((z.Q, z.LV)), dma((z.Q, z.LV)),
-        dma((z.ND,)), dma((z.ND,)), dma((z.ND,)), dma((z.ND,)),
-        dma((halves,)), dma((halves,)), dma((1,)), dma((z.B * z.Q,)), dma((halves,)), dma((1,)),
     ]
-    grad_state, grads = pl.pallas_call(
-        functools.partial(kernel, z),
+    reduce_sems = [dma((z.ND,))] * 4
+    if z.joint:
+        body = joint_kernel
+        block = (z.ND, z.Q, z.RP * z.JQ, z.C)
+        buf = pltpu.VMEM(block, BF16)
+        obs_buf = (z.LV, z.JD, z.F, z.O)
+        flat = pltpu.VMEM((z.ND * z.RP * z.JQ, z.C), F32)
+        columns = pltpu.VMEM((z.JD, z.F, lon), BF16)
+        pair = dma((z.Q, z.ND))
+        scratch = weights + [
+            pltpu.VMEM((z.R, z.ND * z.JD, z.N), BF16),
+            pltpu.VMEM((z.RP, z.C, z.N), F32),
+            buf, buf, buf, pltpu.VMEM((2,) + block, BF16), buf, buf,
+            pltpu.VMEM(obs_buf, BF16), pltpu.VMEM((2,) + obs_buf, BF16),
+            columns, columns, flat, flat,
+        ] + stages + [
+            pair, pair, pair, dma((2, z.Q, z.ND)), pair, pair,
+            dma((z.LV,)), dma((2, z.LV)),
+        ] + reduce_sems + [
+            dma((halves,)), dma((halves,)), dma((1,)), dma((1,)), dma((1,)), dma((1,)),
+        ]
+    else:
+        body = kernel
+        band_buf = pltpu.VMEM((z.B, z.Q, z.RP, z.JJ, z.C), BF16)
+        lev_buf = pltpu.VMEM((z.LV, z.Q, z.JJ, z.VL, z.O), BF16)
+        flat = pltpu.VMEM((z.RT * z.PITCH, z.C), F32)
+        scratch = weights + [
+            pltpu.VMEM((z.R, z.Q, z.B * z.JJ, z.N), BF16),
+            pltpu.VMEM((z.RP, z.C, z.N), F32),
+            band_buf, band_buf, band_buf,
+            pltpu.VMEM((2, z.B, z.Q, z.RP, z.JJ, z.C), BF16),
+            band_buf, band_buf,
+            lev_buf, lev_buf, lev_buf, lev_buf, lev_buf, lev_buf,
+            flat, flat,
+        ] + stages + [
+            dma((z.Q, z.B)), dma((z.Q, z.B)), dma((z.Q, z.B)), dma((2, z.Q, z.B)),
+            dma((z.Q, z.B)), dma((z.Q, z.B)),
+            dma((z.Q, z.LV)), dma((z.Q, z.LV)), dma((z.Q, z.LV)), dma((z.Q, z.LV)),
+            dma((z.Q, z.LV)), dma((z.Q, z.LV)),
+        ] + reduce_sems + [
+            dma((halves,)), dma((halves,)), dma((1,)), dma((z.B * z.Q,)), dma((1,)), dma((1,)),
+        ]
+    state, grads = pl.pallas_call(
+        functools.partial(body, z),
         out_shape=[
-            jax.ShapeDtypeStruct((z.ROWS, z.N), F32),
+            jax.ShapeDtypeStruct((z.RP, z.C, z.N), F32),
             jax.ShapeDtypeStruct((z.ND, 3, z.HD, z.F), BF16),
         ],
-        in_specs=[any_space] * 4 + [smem] * 2 + [vmem] * 7,
+        in_specs=[any_space] * 4 + [smem] * 2 + [vmem] * 3,
         out_specs=[any_space, any_space],
         scratch_shapes=scratch,
         compiler_params=pltpu.CompilerParams(
@@ -546,17 +1044,26 @@
         final_cot.reshape(z.ROWS, z.N),
         obs_cot.reshape(z.NO, z.F, z.J, z.O),
         legendre,
-        obs_time, wave_order, damp, tab_t, tab_w,
-        w_in_p.T, w_in_p, w_out_p,
-        jnp.broadcast_to(bias[:, None], (z.H, z.O)),
+        obs_time, wave_order, w_in, w_out, bias[None],
     )
-    grads = jnp.swapaxes(grads, 0, 1).astype(F32).reshape(3, z.H, z.F)
-    return (
-        grad_state.reshape(final_cot.shape),
-        from_wire(grads[0].T, 0),
-        from_wire(grads[1], 1),
-        jnp.sum(grads[2], axis=1),
-    )
+    grad_state, grad_in, grad_out, grad_bias = pl.pallas_call(
+        functools.partial(finish, z),
+        out_shape=[
+            jax.ShapeDtypeStruct((z.ROWS, z.N), F32),
+            jax.ShapeDtypeStruct((z.F, z.H), F32),
+            jax.ShapeDtypeStruct((z.H, z.F), F32),
+            jax.ShapeDtypeStruct((1, z.H), F32),
+        ],
+        in_specs=[vmem, vmem],
+        out_specs=[any_space, vmem, vmem, vmem],
+        scratch_shapes=[
+            pltpu.VMEM((halves, z.ROWS, LANES), F32),
+            pltpu.VMEM((3, z.H, z.F), F32),
+            dma((halves,)),
+        ],
+        compiler_params=pltpu.CompilerParams(vmem_limit_bytes=40 * 1024 * 1024),
+    )(state, grads)
+    return grad_state.reshape(final_cot.shape), grad_in, grad_out, grad_bias[0]
 
 
 def solution(mesh):

time: 367 us -> 321 us (0.87)
  Pallas kernels: 344 us -> 316 us
  local copies, waits for them, and re-layouts: 14.1 us -> 2.58 us
  other arithmetic: 7 us -> 0 us
    pallas_call x1 -> x2, Pallas kernels: 344 us -> 316 us  [the longest x1 312 us: shards(): pl.pallas_call(functools.partial(body, z), out_shape=[jax.ShapeDtypeStruc...]
where the time goes in v2:
time: 321 us; the launch traced here: 320 us
  Pallas kernels  316 us (98%)
    pallas_call x1, Pallas kernels, shards(): pl.pallas_call(functools.partial(body, z), out_shape=[jax.ShapeDtypeStruc...  312 us

profile of v2, /device:TPU:1, one launch (start us, length us, event | category | flops | bytes accessed | tf_op | source)
XLA Modules:
  0.0 319.7 jit_solution(881867508398513540)
XLA Ops:
  0.6 312.4 %shard_map.120 = (f32[16,128,256]{2,1,0:T(8,128)}, bf16[32,3,16,128]{3,2,1,0:T(8,128)(2,1)}) custom-call(f32[4,2048,256]{2,1,0:T(8,128)} %bitcast.6, f32[2048,256]{1,0:T(8,128)} %bitcast.8, f32[4,128,32,128]{3,2,1,0:T(8,128)} %bitcast.7, bf16[32,256,256]{2,1,0:T(8,128)(2,1)} %leg.1, s32[4]{0:T(128)} %obs_time.1, s32[256]{0:T(256)} %wave.1, ...), custom_call_target="tpu_custom_call" | custom-call | tf_op jit(solution)/shard_map/pallas_call | solution.py:1031
  313.0 0.0 copy-start
  313.0 1.6 copy-done
  314.6 0.0 copy-start.1
  314.6 1.0 copy-done.1
  315.6 4.1 %shard_map.121 = (f32[2048,256]{1,0:T(8,128)}, f32[128,512]{1,0:T(8,128)}, f32[512,128]{1,0:T(8,128)}, f32[1,512]{1,0:T(1,128)}) custom-call(f32[16,128,256]{2,1,0:T(8,128)S(1)} %copy-done, bf16[32,3,16,128]{3,2,1,0:T(8,128)(2,1)S(1)} %copy-done.1), custom_call_target="tpu_custom_call" | custom-call | tf_op jit(solution)/shard_map/pallas_call | solution.py:1049
Async XLA Ops:
  313.0 1.6 copy-start
  314.6 1.0 copy-start.1

commit v3 on v2

--- a/solution.py
+++ b/solution.py
@@ -29,6 +29,7 @@
         self.J, self.O, self.H = lat, lon, hidden
         self.RP = waves // 2
         self.RT = self.RP * bands
+        self.PR = 2 * waves + 8
         self.JJ = min(16, lat)
         self.Q = lat // self.JJ
         self.VL = fields * levels
@@ -519,8 +520,8 @@
     tab_t, tab_w, w_in_t, w_in, w_out, bias, orders, damp,
     tab, adj, tsend, trecv, fsend, frecv, bsend, brecv, osend, orecv,
     feats, tangs, fs, fs2, cstage, ostage, obs_all, obs_s, acc_in, acc_out, acc_b,
-    rs_send, rs_recv, ag_send, ag_recv,
-    t_s, t_r, f_s, f_r, b_s, b_r, o_s, o_r, rs_s, rs_r, ag_s, ag_r,
+    rs_send, rs_recv, rb_send, rb_recv, ag_send, gb_recv, ag_recv,
+    t_s, t_r, f_s, f_r, b_s, b_r, o_s, o_r, rl_s, rl_r, rb_s, rb_r,
     ck_sem, fc_sem, obs_sem, leg_sem, out_sem, g_sem,
 ):
     me_b = lax.axis_index("band")
@@ -572,21 +573,26 @@
             osend.at[v], orecv.at[0, v], o_s.at[v], o_r.at[0, v],
             me_b * z.LV + v).wait_send())
 
-    def ck_copy(k, h):
-        return pltpu.make_async_copy(
-            ck.at[k, :, pl.ds(h * LANES, LANES)], cstage.at[h], ck_sem.at[h])
-
-    def fc_copy(h):
-        return pltpu.make_async_copy(
-            fc.at[:, pl.ds(h * LANES, LANES)], ostage.at[h], fc_sem.at[h])
+    def stage_copies(src, stage, sem, h):
+        def copy(v, _):
+            pltpu.make_async_copy(
+                src.at[pl.ds(v * 2 * z.R, 2 * z.R), pl.ds(h * LANES, LANES)],
+                stage.at[h, pl.ds(v * z.PR, 2 * z.R)], sem.at[h]).start()
+            return 0
+
+        lax.fori_loop(0, z.VL, copy, 0)
+
+    def stage_wait(src, stage, sem, h):
+        pltpu.make_async_copy(
+            src.at[:, pl.ds(h * LANES, LANES)], stage.at[h, pl.ds(0, z.ROWS)], sem.at[h]).wait()
 
     leg_copy = pltpu.make_async_copy(leg, tab, leg_sem.at[0])
     obs_copy = pltpu.make_async_copy(obs, obs_all, obs_sem.at[0])
     for h in range(halves):
-        ck_copy(z.S - 1, h).start()
+        stage_copies(ck.at[z.S - 1], cstage, ck_sem, h)
     leg_copy.start()
     for h in range(halves):
-        fc_copy(h).start()
+        stage_copies(fc, ostage, fc_sem, h)
     obs_copy.start()
 
     degree = lax.broadcasted_iota(jnp.int32, (half_c, z.N), 1)
@@ -600,7 +606,7 @@
             for p in range(2):
                 start = p * z.R + 2 * rp + r2
                 parts.append(jnp.concatenate(
-                    [stage[h, pl.ds(start, z.VL, stride=2 * z.R), :] for h in range(halves)], axis=1))
+                    [stage[h, pl.ds(start, z.VL, stride=z.PR), :] for h in range(halves)], axis=1))
         return jnp.concatenate(parts, axis=0)
 
     lat = z.ND * z.JD
@@ -771,32 +777,63 @@
                     tab_t[rows, cols] = value
                     tab_w[rows, cols] = (value.astype(F32) * weight).astype(BF16)
 
-    def reduce_send():
+    def lev_copy(src, dst, stage, mine, v):
+        return remote(src, dst, rl_s.at[stage, v], rl_r.at[stage, mine], me_b * z.LV + v)
+
+    def band_copy(src, dst, stage, mine, b):
+        return remote(src, dst, rb_s.at[stage, b], rb_r.at[stage, mine], b * z.LV + me_l)
+
+    def reduce_lev():
         for i, acc in enumerate((acc_in, acc_out, acc_b)):
-            for d in range(z.ND):
-                rs_send[d, i] = acc[d * z.HD:(d + 1) * z.HD].astype(BF16)
-        rs_recv[me] = rs_send[me]
-        others(z.ND, me, lambda d: remote(
-            rs_send.at[d], rs_recv.at[me], rs_s.at[d], rs_r.at[me], d).start())
-
-    def gather_send():
-        others(z.ND, me, lambda d: remote(
-            rs_send.at[d], rs_recv.at[d], rs_s.at[d], rs_r.at[d], d).wait())
-        total = rs_recv[0].astype(F32)
-        for d in range(1, z.ND):
-            total = total + rs_recv[d].astype(F32)
+            for v in range(z.LV):
+                for b in range(z.B):
+                    row = (v * z.B + b) * z.HD
+                    rs_send[v, b, i] = acc[row:row + z.HD].astype(BF16)
+        rs_recv[me_l] = rs_send[me_l]
+        others(z.LV, me_l, lambda v: lev_copy(
+            rs_send.at[v], rs_recv.at[me_l], 0, me_l, v).start())
+
+    def reduce_band():
+        others(z.LV, me_l, lambda v: lev_copy(
+            rs_send.at[v], rs_recv.at[v], 0, v, v).wait())
+
+        def add(b, _):
+            total = rs_recv[0, b].astype(F32)
+            for v in range(1, z.LV):
+                total = total + rs_recv[v, b].astype(F32)
+            rb_send[b] = total.astype(BF16)
+            return 0
+
+        lax.fori_loop(0, z.B, add, 0)
+        rb_recv[me_b] = rb_send[me_b]
+        others(z.B, me_b, lambda b: band_copy(
+            rb_send.at[b], rb_recv.at[me_b], 0, me_b, b).start())
+
+    def gather_band():
+        others(z.B, me_b, lambda b: band_copy(
+            rb_send.at[b], rb_recv.at[b], 0, b, b).wait())
+        total = rb_recv[0].astype(F32)
+        for b in range(1, z.B):
+            total = total + rb_recv[b].astype(F32)
         total = total.astype(BF16)
         ag_send[...] = total
-        ag_recv[me] = total
-        others(z.ND, me, lambda d: remote(
-            ag_send, ag_recv.at[me], ag_s.at[d], ag_r.at[me], d).start())
+        gb_recv[me_b] = total
+        others(z.B, me_b, lambda b: band_copy(
+            ag_send, gb_recv.at[me_b], 1, me_b, b).start())
+
+    def gather_lev():
+        others(z.B, me_b, lambda b: band_copy(
+            ag_send, gb_recv.at[b], 1, b, b).wait())
+        ag_recv[me_l] = gb_recv[...]
+        others(z.LV, me_l, lambda v: lev_copy(
+            gb_recv, ag_recv.at[me_l], 1, me_l, v).start())
 
     def gather_wait():
-        others(z.ND, me, lambda d: remote(
-            ag_send, ag_recv.at[d], ag_s.at[d], ag_r.at[d], d).wait())
+        others(z.LV, me_l, lambda v: lev_copy(
+            gb_recv, ag_recv.at[v], 1, v, v).wait())
 
     for h in range(halves):
-        ck_copy(z.S - 1, h).wait()
+        stage_wait(ck.at[z.S - 1], cstage, ck_sem, h)
     leg_copy.wait()
     tang = (tsend, trecv, t_s, t_r)
     back = (bsend, brecv, b_s, b_r)
@@ -809,11 +846,11 @@
     send_all(*feat(first), 0)
     if z.S > 1:
         for h in range(halves):
-            ck_copy(z.S - 2, h).start()
+            stage_copies(ck.at[z.S - 2], cstage, ck_sem, h)
     degrees = lax.broadcasted_iota(jnp.int32, (1, z.N), 1).astype(F32)
     damp[...] = 1.0 / (1.0 + 2.0 * degrees * (degrees + 1.0) / (z.N * z.N))
     for h in range(halves):
-        fc_copy(h).wait()
+        stage_wait(fc, ostage, fc_sem, h)
 
     def initial(rp, _):
         adj[rp] = rows_of(ostage, rp)
@@ -852,6 +889,11 @@
                 wait_send(*back, q)
 
             network(q, par)
+            if q == z.Q - 1:
+                @pl.when(k == 0)
+                def _():
+                    reduce_lev()
+
             send_all(*back, q)
 
         do_f(0)
@@ -859,7 +901,7 @@
         @pl.when(k > 0)
         def _():
             for h in range(halves):
-                ck_copy(k - 1, h).wait()
+                stage_wait(ck.at[k - 1], cstage, ck_sem, h)
             for q in range(z.Q):
                 wait_send(*feat(0), q)
             features_legendre()
@@ -868,7 +910,7 @@
         @pl.when(k > 1)
         def _():
             for h in range(halves):
-                ck_copy(k - 2, h).start()
+                stage_copies(ck.at[k - 2], cstage, ck_sem, h)
 
         do_n(0)
 
@@ -882,10 +924,6 @@
             do_f(q)
             do_n(q)
 
-        @pl.when(k == 0)
-        def _():
-            reduce_send()
-
         @pl.when(k > 0)
         def _():
             for q in range(1, z.Q):
@@ -893,10 +931,15 @@
 
         @pl.when(k == 0)
         def _():
-            gather_send()
+            reduce_band()
 
         for q in range(z.Q):
             wait_recv(*back, q)
+
+        @pl.when(k == 0)
+        def _():
+            gather_band()
+
         adjoint_legendre()
         for q in range(z.Q):
             wait_send(*tang, q)
@@ -912,6 +955,7 @@
     lax.fori_loop(0, z.S, step, 0)
     adj_copy = pltpu.make_async_copy(adj, out, out_sem.at[0])
     adj_copy.start()
+    gather_lev()
     gather_wait()
     gather_copy = pltpu.make_async_copy(ag_recv, gout, g_sem.at[0])
     gather_copy.start()
@@ -923,25 +967,39 @@
     gather_copy.wait()
 
 
-def finish(z, adj, grads, out, grad_in, grad_out, grad_bias, stage, flat, sem):
+def finish(z, adj_hbm, grads_hbm, out, grad_in, grad_out, grad_bias, adj, grads, stage, flat, sem, in_sem):
     half_c = 2 * z.VL
-    copies = []
-    for h in range(z.N // LANES):
-        cols = slice(h * LANES, (h + 1) * LANES)
+    halves = z.N // LANES
+    grads_copy = pltpu.make_async_copy(grads_hbm, grads, in_sem.at[halves])
+    adj_copies = [
+        pltpu.make_async_copy(adj_hbm.at[:, :, pl.ds(h * LANES, LANES)], adj.at[h], in_sem.at[h])
+        for h in range(halves)
+    ]
+    for copy in adj_copies:
+        copy.start()
+    grads_copy.start()
+    for h in range(halves):
+        adj_copies[h].wait()
 
         def body(rp, _):
             for r2 in range(2):
                 for p in range(2):
                     start = p * z.R + 2 * rp + r2
                     c = r2 * half_c + p * z.VL
-                    stage[h, pl.ds(start, z.VL, stride=2 * z.R), :] = adj[rp, c:c + z.VL, cols]
-            return 0
-
-        lax.fori_loop(0, z.RP, body, 0)
-        copy = pltpu.make_async_copy(stage.at[h], out.at[:, pl.ds(h * LANES, LANES)], sem.at[h])
-        copy.start()
-        copies.append(copy)
-
+                    stage[h, pl.ds(start, z.VL, stride=z.PR), :] = adj[h, rp, c:c + z.VL]
+            return 0
+
+        lax.fori_loop(0, z.RP, body, 0, unroll=2)
+
+        def store(v, _):
+            pltpu.make_async_copy(
+                stage.at[h, pl.ds(v * z.PR, 2 * z.R)],
+                out.at[pl.ds(v * 2 * z.R, 2 * z.R), pl.ds(h * LANES, LANES)], sem.at[h]).start()
+            return 0
+
+        lax.fori_loop(0, z.VL, store, 0)
+
+    grads_copy.wait()
     for d in range(z.ND):
         for i in range(3):
             flat[i, d * z.HD:(d + 1) * z.HD] = grads[d, i].astype(F32)
@@ -954,8 +1012,9 @@
     grad_in[...] = from_wire(flat[0].T)
     grad_out[...] = from_wire(flat[1].T).T
     grad_bias[...] = jnp.sum(flat[2].T, axis=0, keepdims=True)
-    for copy in copies:
-        copy.wait()
+    for h in range(halves):
+        pltpu.make_async_copy(
+            stage.at[h, pl.ds(0, z.ROWS)], out.at[:, pl.ds(h * LANES, LANES)], sem.at[h]).wait()
 
 
 def shards(checkpoints, final_cot, obs_cot, obs_time, wave_order, legendre, w_in, w_out, bias):
@@ -977,18 +1036,21 @@
         pltpu.VMEM((z.H, z.F), BF16), pltpu.VMEM((z.F, z.H), BF16), pltpu.VMEM((z.H, z.F), BF16),
         pltpu.VMEM((z.H, z.O), F32), pltpu.VMEM((2 * z.RT, LANES), jnp.int32), pltpu.VMEM((1, z.N), F32),
     ]
+    stage_rows = z.VL * z.PR if z.joint else z.ROWS
     stages = [
-        pltpu.VMEM((halves, z.ROWS, LANES), F32),
-        pltpu.VMEM((halves, z.ROWS, LANES), F32),
+        pltpu.VMEM((halves, stage_rows, LANES), F32),
+        pltpu.VMEM((halves, stage_rows, LANES), F32),
         pltpu.VMEM((z.NO, z.F, z.J, z.O), F32),
         pltpu.VMEM((z.J * z.OPITCH, z.O), F32),
         pltpu.VMEM((z.H, z.F), F32), pltpu.VMEM((z.H, z.F), F32), pltpu.VMEM((z.H, z.O), F32),
-        reduce_buf, reduce_buf,
-        pltpu.VMEM((3, z.HD, z.F), BF16), reduce_buf,
     ]
-    reduce_sems = [dma((z.ND,))] * 4
+    part = pltpu.VMEM((3, z.HD, z.F), BF16)
+    grads_shape = (z.ND, 3, z.HD, z.F)
     if z.joint:
         body = joint_kernel
+        grads_shape = (z.LV, z.B, 3, z.HD, z.F)
+        reduce_buf = pltpu.VMEM(grads_shape, BF16)
+        band_part = pltpu.VMEM(grads_shape[1:], BF16)
         block = (z.ND, z.Q, z.RP * z.JQ, z.C)
         buf = pltpu.VMEM(block, BF16)
         obs_buf = (z.LV, z.JD, z.F, z.O)
@@ -1002,9 +1064,10 @@
             pltpu.VMEM(obs_buf, BF16), pltpu.VMEM((2,) + obs_buf, BF16),
             columns, columns, flat, flat,
         ] + stages + [
+            reduce_buf, reduce_buf, band_part, band_part, part, band_part, reduce_buf,
             pair, pair, pair, dma((2, z.Q, z.ND)), pair, pair,
             dma((z.LV,)), dma((2, z.LV)),
-        ] + reduce_sems + [
+            dma((2, z.LV)), dma((2, z.LV)), dma((2, z.B)), dma((2, z.B)),
             dma((halves,)), dma((halves,)), dma((1,)), dma((1,)), dma((1,)), dma((1,)),
         ]
     else:
@@ -1021,18 +1084,19 @@
             lev_buf, lev_buf, lev_buf, lev_buf, lev_buf, lev_buf,
             flat, flat,
         ] + stages + [
+            reduce_buf, reduce_buf, part, reduce_buf,
             dma((z.Q, z.B)), dma((z.Q, z.B)), dma((z.Q, z.B)), dma((2, z.Q, z.B)),
             dma((z.Q, z.B)), dma((z.Q, z.B)),
             dma((z.Q, z.LV)), dma((z.Q, z.LV)), dma((z.Q, z.LV)), dma((z.Q, z.LV)),
             dma((z.Q, z.LV)), dma((z.Q, z.LV)),
-        ] + reduce_sems + [
+            dma((z.ND,)), dma((z.ND,)), dma((z.ND,)), dma((z.ND,)),
             dma((halves,)), dma((halves,)), dma((1,)), dma((z.B * z.Q,)), dma((1,)), dma((1,)),
         ]
     state, grads = pl.pallas_call(
         functools.partial(body, z),
         out_shape=[
             jax.ShapeDtypeStruct((z.RP, z.C, z.N), F32),
-            jax.ShapeDtypeStruct((z.ND, 3, z.HD, z.F), BF16),
+            jax.ShapeDtypeStruct(grads_shape, BF16),
         ],
         in_specs=[any_space] * 4 + [smem] * 2 + [vmem] * 3,
         out_specs=[any_space, any_space],
@@ -1054,15 +1118,17 @@
             jax.ShapeDtypeStruct((z.H, z.F), F32),
             jax.ShapeDtypeStruct((1, z.H), F32),
         ],
-        in_specs=[vmem, vmem],
+        in_specs=[any_space, any_space],
         out_specs=[any_space, vmem, vmem, vmem],
         scratch_shapes=[
-            pltpu.VMEM((halves, z.ROWS, LANES), F32),
+            pltpu.VMEM((halves, z.RP, z.C, LANES), F32),
+            pltpu.VMEM((z.ND, 3, z.HD, z.F), BF16),
+            pltpu.VMEM((halves, z.VL * z.PR, LANES), F32),
             pltpu.VMEM((3, z.H, z.F), F32),
-            dma((halves,)),
+            dma((halves,)), dma((halves + 1,)),
         ],
         compiler_params=pltpu.CompilerParams(vmem_limit_bytes=40 * 1024 * 1024),
-    )(state, grads)
+    )(state, grads.reshape(z.ND, 3, z.HD, z.F))
     return grad_state.reshape(final_cot.shape), grad_in, grad_out, grad_bias[0]
 
 

time: 321 us -> 312 us (0.972)
  Pallas kernels: 316 us -> 309 us
    pallas_call x1, Pallas kernels: 312 us -> 306 us  [shards(): pl.pallas_call(functools.partial(body, z), out_shape=[jax.ShapeDtypeStruc...]
where the time goes in v3:
time: 312 us
  Pallas kernels  309 us (99%)
    pallas_call x1, Pallas kernels, shards(): pl.pallas_call(functools.partial(body, z), out_shape=[jax.ShapeDtypeStruc...  306 us

profile of v3, /device:TPU:1, one launch (start us, length us, event | category | flops | bytes accessed | tf_op | source)
XLA Modules:
  0.0 312.2 jit_solution(3242308571366323836)
XLA Ops:
  0.6 306.1 %shard_map.120 = (f32[16,128,256]{2,1,0:T(8,128)}, bf16[4,8,3,16,128]{4,3,2,1,0:T(8,128)(2,1)}) custom-call(f32[4,2048,256]{2,1,0:T(8,128)} %bitcast.8, f32[2048,256]{1,0:T(8,128)} %bitcast.10, f32[4,128,32,128]{3,2,1,0:T(8,128)} %bitcast.9, bf16[32,256,256]{2,1,0:T(8,128)(2,1)} %leg.1, s32[4]{0:T(128)} %obs_time.1, s32[256]{0:T(256)} %wave.1, ...), custom_call_target="tpu_custom_call" | custom-call | tf_op jit(solution)/shard_map/pallas_call | solution.py:1095
  306.7 0.0 copy-start
  306.8 1.6 copy-done
  308.3 0.0 copy-start.1
  308.3 1.0 copy-done.1
  309.3 2.8 shard_map.121
Async XLA Ops:
  306.7 1.6 copy-start
  308.3 1.0 copy-start.1

commit v4 on v3

--- a/solution.py
+++ b/solution.py
@@ -536,7 +536,7 @@
             body(lax.rem(own + d, count))
             return 0
 
-        lax.fori_loop(1, count, step, 0)
+        lax.fori_loop(1, count, step, 0, unroll=min(4, count - 1))
 
     def remote(src, dst, ssem, rsem, d):
         return pltpu.make_async_remote_copy(

time: 312 us -> 311 us (level)
  no operation moved by 1% of the time
where the time goes in v4:
time: 311 us
  Pallas kernels  307 us (99%)
    pallas_call x1, Pallas kernels, shards(): pl.pallas_call(functools.partial(body, z), out_shape=[jax.ShapeDtypeStruc...  305 us

profile of v4, /device:TPU:1, one launch (start us, length us, event | category | flops | bytes accessed | tf_op | source)
XLA Modules:
  0.0 310.7 jit_solution(16997099344668898170)
XLA Ops:
  0.6 304.6 %shard_map.120 = (f32[16,128,256]{2,1,0:T(8,128)}, bf16[4,8,3,16,128]{4,3,2,1,0:T(8,128)(2,1)}) custom-call(f32[4,2048,256]{2,1,0:T(8,128)} %bitcast.8, f32[2048,256]{1,0:T(8,128)} %bitcast.10, f32[4,128,32,128]{3,2,1,0:T(8,128)} %bitcast.9, bf16[32,256,256]{2,1,0:T(8,128)(2,1)} %leg.1, s32[4]{0:T(128)} %obs_time.1, s32[256]{0:T(256)} %wave.1, ...), custom_call_target="tpu_custom_call" | custom-call | tf_op jit(solution)/shard_map/pallas_call | solution.py:1095
  305.2 0.0 copy-start
  305.3 1.6 copy-done
  306.8 0.0 copy-start.1
  306.8 1.0 copy-done.1
  307.8 2.8 shard_map.121
Async XLA Ops:
  305.2 1.6 copy-start
  306.8 1.0 copy-start.1
